TPU v7x, 512 devices: a whole 4x4x16 slice. The times are simulated.
512 devices in a mesh: mem: 8 (over y, core), space: 64 (over x, z).
Axes of the slice: x: 4, y: 4, z: 16, core: 2. Of those that a mesh axis runs over, the one named last changes fastest.
Arguments:
- members: float32 [64, 1024, 1024], P('mem', 'space'), may hold values from -6 to 6
- flow_east: float32 [1024, 1024], P('space'), may hold values from -0.2 to 0.2
- flow_north: float32 [1024, 1024], P('space'), may hold values from -0.2 to 0.2
- mixing: float32 [1024, 1024], P('space'), may hold values from 0.05 to 0.24
- land_mask: int32 [1024, 1024], P('space'), may hold values 0 or 1
- sensor_cell: int32 [131072], P('space'), may hold values from 0 to 16383, as said below
- sensor_value: float32 [131072], P('space'), may hold values from -6 to 6
- sensor_noise: float32 [131072], P('space'), may hold values from 0.25 to 4
- tile_lists: int32 [1024, 8, 256], P('space', 'mem'), may hold values from 0 to 6143, as said below
- tile_counts: int32 [1024, 8], P('space', 'mem'), may hold values from 0 to 256, as said below
Outputs:
- analysis: float32 [64, 1024, 1024], P(None, 'space', 'mem')
Inputs may be any that keep to these rules, and one draw needn't show every extreme that they name: Sensor j belongs to strip j // 2048: sensor_cell[j] // 1024 is its row within the strip's 16 rows and sensor_cell[j] % 1024 its column. `tile_lists`: for a tile in strip t an entry e names sensor (t - 1) * 2048 + e; the used entries of a tile are distinct sensors that exist, within 16 cells of the tile. `tile_counts`: at most 256, reached by some tile of every strip in every draw.
All inputs are finite; a program needn't handle non-finite values. No bound on the sum of `land_mask` on one device may be relied on, other than what follows from the above.
Results may differ from a plain program's by a relative error of at most 0.0003.
Values sent between devices are 32-bit elements; how exact they have to be, the bound alone decides.
A program may use at most 64 MiB of HBM per device.

v0:
```python
import jax
import jax.numpy as jnp
from jax import lax
from jax.sharding import Mesh
from jax.sharding import PartitionSpec as P

TW = 128
STEPS = 4
NSITER = 8
RLOC = 8
MEM = ("mem_0", "mem_1")


highest = lax.Precision.HIGHEST


def with_halo(cells, sides, width):
    for axis, dim in sides:
        count = lax.axis_size(axis)
        ends = count - 1
        head = lax.slice_in_dim(cells, 0, width, axis=dim)
        tail = lax.slice_in_dim(cells, cells.shape[dim] - width, cells.shape[dim], axis=dim)
        cells = jnp.concatenate(
            [
                lax.ppermute(tail, axis, [(i, (i + 1) % count) for i in range(ends)]),
                cells,
                lax.ppermute(head, axis, [((i + 1) % count, i) for i in range(ends)]),
            ],
            axis=dim,
        )
    return cells


def copy_for_each(value, axis):
    copies = jnp.broadcast_to(value, (lax.axis_size(axis), *value.shape))
    return lax.all_to_all(copies, axis, split_axis=0, concat_axis=0, tiled=True)


def joined_along(tiles, dim):
    dims = list(tiles.shape[1:])
    dims[dim] *= tiles.shape[0]
    return jnp.moveaxis(tiles, 0, dim).reshape(dims)


def gather_directly(value, axis, dim):
    tiles = copy_for_each(value, axis)
    return joined_along(tiles, dim)


def in_blocks(value, dim, length):
    dims = value.shape
    tiles = value.reshape(*dims[:dim], length, dims[dim] // length, *dims[dim + 1 :])
    return jnp.moveaxis(tiles, dim, 0)


def exchange_in_order(tiles, axes, sequence):
    inside = tiles.shape[1:]
    filled = tiles.reshape(*(lax.axis_size(a) for a in axes), *inside)
    for k in sequence:
        filled = lax.all_to_all(filled, axes[k], k, k, tiled=True)
    return filled.reshape(-1, *inside)


def two_step_exchange(value, groups, sequence, split_dim, concat_dim):
    length = lax.axis_size(groups[0]) * lax.axis_size(groups[1])
    tiles = in_blocks(value, split_dim, length)
    return joined_along(exchange_in_order(tiles, groups, sequence), concat_dim)


def gaspari(ratio):
    capped = jnp.maximum(ratio, 1.0)
    inner = (((-0.25 * ratio + 0.5) * ratio + 0.625) * ratio - 5.0 / 3.0) * ratio * ratio + 1.0
    outer = (
        ((((ratio / 12.0 - 0.5) * ratio + 0.625) * ratio + 5.0 / 3.0) * ratio - 5.0) * ratio
        + 4.0
        - 2.0 / (3.0 * capped)
    )
    return jnp.where(ratio <= 1.0, inner, jnp.where(ratio <= 2.0, outer, 0.0))


def advance(padded, flow_east, flow_north, mixing, ocean):
    centre = padded[:, 1:-1, :]
    northern = padded[:, 2:, :]
    southern = padded[:, :-2, :]
    eastern = jnp.roll(centre, -1, axis=2)
    western = jnp.roll(centre, 1, axis=2)
    carried = 0.5 * flow_east * (eastern - western) + 0.5 * flow_north * (northern - southern)
    spread = eastern + western + northern + southern - 4.0 * centre
    return ocean * (centre - carried + mixing * spread)


def analyse(
    ensemble,
    values,
    variance,
    sensor_row,
    sensor_col,
    usable,
    tile_row,
    tile_mid,
    fields,
    width_total,
):
    count_members = ensemble.shape[0]
    prior_mean = jnp.mean(ensemble, axis=0)
    spread = ensemble - prior_mean
    depart = values - prior_mean
    offset_rows = sensor_row - tile_row[:, None]
    offset_cols = jnp.abs(sensor_col - tile_mid[:, None])
    offset_cols = jnp.minimum(offset_cols, width_total - offset_cols)
    offset_cols = jnp.maximum(offset_cols - (TW - 1) / 2.0, 0.0)
    distance = jnp.sqrt(offset_cols * offset_cols + offset_rows * offset_rows)
    safe_variance = jnp.where(usable, variance, 1.0)
    weight = jnp.where(usable, gaspari(distance / RLOC) / safe_variance, 0.0)
    gram_matrix = jnp.einsum("knl,jnl->nkj", spread * weight, spread, precision=highest)
    identity = jnp.eye(count_members, dtype=jnp.float32)
    normed = identity + gram_matrix / (count_members - 1)
    frobenius = jnp.sqrt(jnp.sum(normed * normed, axis=(1, 2)))
    iterate = normed / frobenius[:, None, None]
    inverse_root = jnp.broadcast_to(identity, normed.shape)
    for repeat in range(NSITER):
        factor = 1.5 * identity - 0.5 * jnp.matmul(inverse_root, iterate, precision=highest)
        iterate = jnp.matmul(iterate, factor, precision=highest)
        inverse_root = jnp.matmul(factor, inverse_root, precision=highest)
    transform = inverse_root / jnp.sqrt(frobenius)[:, None, None]
    forcing = jnp.einsum("knl,nl->nk", spread, weight * depart, precision=highest)
    halfway = jnp.einsum("nkj,nj->nk", transform, forcing, precision=highest)
    shift_mean = jnp.einsum("nkj,nj->nk", transform, halfway, precision=highest) / (
        count_members - 1
    )
    mixture = transform + shift_mean[:, :, None]
    field_mean = jnp.mean(fields, axis=0)
    return field_mean + jnp.einsum("njk,jnc->knc", mixture, fields - field_mean, precision=highest)


def body(
    members,
    flow_east,
    flow_north,
    mixing,
    land_mask,
    sensor_cell,
    sensor_value,
    sensor_noise,
    tile_lists,
    tile_counts,
):
    ocean = land_mask.astype(jnp.float32)
    fields = members * ocean
    rows_here = members.shape[1]
    width_total = members.shape[2]
    coeffs = jnp.stack([flow_east, flow_north, mixing, ocean])
    extended, coeff_rows = (
        with_halo(fields, (("space", 1),), STEPS),
        with_halo(coeffs, (("space", 1),), STEPS),
    )
    for repeat in range(STEPS):
        upper = rows_here + 2 * STEPS - repeat - 1
        extended = advance(
            extended,
            coeff_rows[0, repeat + 1 : upper],
            coeff_rows[1, repeat + 1 : upper],
            coeff_rows[2, repeat + 1 : upper],
            coeff_rows[3, repeat + 1 : upper],
        )
    fields = extended
    space_index = lax.axis_index("space")
    mem_index = lax.axis_index(MEM)
    flattened = fields.reshape(fields.shape[0], rows_here * width_total)
    readings = jnp.take(flattened, sensor_cell, axis=1)
    sensor_row = (space_index * rows_here + sensor_cell // width_total).astype(jnp.float32)
    sensor_col = (sensor_cell % width_total).astype(jnp.float32)
    details = jnp.stack([sensor_value, sensor_noise, sensor_row, sensor_col])
    everyone = gather_directly(readings, MEM, 0)
    pooled, near_details = (
        with_halo(everyone, (("space", 1),), readings.shape[1]),
        with_halo(details, (("space", 1),), readings.shape[1]),
    )
    columns = two_step_exchange(fields, ("mem_0", "mem_1"), (0, 1), 2, 0)
    count_members = pooled.shape[0]
    slot_index = jnp.arange(tile_lists.shape[2], dtype=jnp.int32)
    chosen = tile_lists[:, 0, :]
    usable = slot_index[None, :] < tile_counts[:, 0][:, None]
    combined = jnp.concatenate([pooled, near_details], axis=0)
    selected = jnp.take(combined, chosen, axis=1)
    ensemble = selected[:count_members]
    picked = selected[count_members:]
    tile_row = (space_index * rows_here + jnp.arange(rows_here, dtype=jnp.int32)).astype(
        jnp.float32
    )
    tile_mid = jnp.ones((rows_here,), jnp.float32) * (
        (mem_index * TW).astype(jnp.float32) + (TW - 1) / 2.0
    )
    return analyse(
        ensemble,
        picked[0],
        picked[1],
        picked[2],
        picked[3],
        usable,
        tile_row,
        tile_mid,
        columns,
        float(width_total),
    )


def solution(mesh):
    torus = Mesh(mesh.devices.reshape(4, 2, mesh.shape["space"]), ("mem_0", "mem_1", "space"))
    in_specs = (
        P(MEM, "space", None),
        P("space", None),
        P("space", None),
        P("space", None),
        P("space", None),
        P("space"),
        P("space"),
        P("space"),
        P("space", MEM, None),
        P("space", MEM),
    )
    out_specs = P(None, "space", MEM)
    return jax.shard_map(body, mesh=torus, in_specs=in_specs, out_specs=out_specs, check_vma=False)
```

profile of v0, /device:TPU:14, one launch (start us, length us, event | category | flops | bytes accessed | tf_op | source)
XLA Modules:
  0.0 137.4 jit_solution(17380566027790281898)
XLA Ops:
  1.6 3.8 %collective-permute-start.6 = (f32[4,2048]{1,0:T(4,128)S(1)}, f32[4,2048]{1,0:T(4,128)S(1)}, u32[]{:S(2)}, u32[]{:S(2)}) collective-permute-start(f32[4,2048]{1,0:T(4,128)S(1)} %pad_maximum_fusion.18), channel_id=1, source_target_pairs={{0,1},{1,2},{2,3},{3,4},{4,5},{5,6},{6,7},{7,8},{8,9},{9,10},{10,1... | collective-permute-start | bytes 98312 | tf_op jit(solution)/shard_map/ppermute | solution.py:25
  5.4 9.8 %collective-permute-start.7 = (f32[4,2048]{1,0:T(4,128)S(1)}, f32[4,2048]{1,0:T(4,128)S(1)}, u32[]{:S(2)}, u32[]{:S(2)}) collective-permute-start(f32[4,2048]{1,0:T(4,128)S(1)} %pad_maximum_fusion.18), channel_id=1, source_target_pairs={{1,0},{2,1},{3,2},{4,3},{5,4},{6,5},{7,6},{8,7},{9,8},{10,9},{11,1... | collective-permute-start | bytes 98312 | tf_op jit(solution)/shard_map/ppermute | solution.py:27
  16.9 1.9 %collective-permute-start = (f32[4,4,1024]{2,1,0:T(4,128)S(1)}, f32[4,4,1024]{2,1,0:T(4,128)S(1)}, u32[]{:S(2)}, u32[]{:S(2)}) collective-permute-start(f32[4,4,1024]{2,1,0:T(4,128)S(1)} %get-tuple-element.37), channel_id=1, source_target_pairs={{0,1},{1,2},{2,3},{3,4},{4,5},{5,6},{6,7},{7,8},{8,9},{9,10},{10,1... | collective-permute-start | bytes 196616 | tf_op jit(solution)/shard_map/ppermute | solution.py:25
  18.8 6.0 %collective-permute-start.1 = (f32[4,4,1024]{2,1,0:T(4,128)S(1)}, f32[4,4,1024]{2,1,0:T(4,128)S(1)}, u32[]{:S(2)}, u32[]{:S(2)}) collective-permute-start(f32[4,4,1024]{2,1,0:T(4,128)S(1)} %get-tuple-element.38), channel_id=1, source_target_pairs={{1,0},{2,1},{3,2},{4,3},{5,4},{6,5},{7,6},{8,7},{9,8},{10,9},{11,1... | collective-permute-start | bytes 196616 | tf_op jit(solution)/shard_map/ppermute | solution.py:27
  26.0 1.9 %collective-permute-start.2 = (f32[8,4,1024]{2,1,0:T(4,128)S(1)}, f32[8,4,1024]{2,1,0:T(4,128)S(1)}, u32[]{:S(2)}, u32[]{:S(2)}) collective-permute-start(f32[8,4,1024]{2,1,0:T(4,128)S(1)} %get-tuple-element.23), channel_id=1, source_target_pairs={{0,1},{1,2},{2,3},{3,4},{4,5},{5,6},{6,7},{7,8},{8,9},{9,10},{10,1... | collective-permute-start | bytes 393224 | tf_op jit(solution)/shard_map/ppermute | solution.py:25
  28.1 6.0 %collective-permute-start.3 = (f32[8,4,1024]{2,1,0:T(4,128)S(1)}, f32[8,4,1024]{2,1,0:T(4,128)S(1)}, u32[]{:S(2)}, u32[]{:S(2)}) collective-permute-start(f32[8,4,1024]{2,1,0:T(4,128)S(1)} %get-tuple-element.24), channel_id=1, source_target_pairs={{1,0},{2,1},{3,2},{4,3},{5,4},{6,5},{7,6},{8,7},{9,8},{10,9},{11,1... | collective-permute-start | bytes 393224 | tf_op jit(solution)/shard_map/ppermute | solution.py:27
  35.0 1.6 %collective-permute-done.3 = f32[8,4,1024]{2,1,0:T(4,128)S(1)} collective-permute-done((f32[8,4,1024]{2,1,0:T(4,128)S(1)}, f32[8,4,1024]{2,1,0:T(4,128)S(1)}, u32[]{:S(2)}, u32[]{:S(2)}) %collective-permute-start.3) | collective-permute-done | bytes 131104 | tf_op jit(solution)/shard_map/ppermute | solution.py:27
  40.6 4.6 %copy.68 = f32[8,16,1024]{0,2,1:T(8,128)} copy(f32[8,16,1024]{2,1,0:T(8,128)S(1)} %add_multiply_fusion.3) | data formatting | bytes 1048576 | tf_op jit(solution)/shard_map/mul | solution.py:89
  45.2 8.8 %gather_fusion = f32[2048,8]{1,0:T(8,128)S(1)} fusion(f32[8,16384]{0,1:T(8,128)} %bitcast.144, s32[2048]{0:T(1024)S(1)} %get-tuple-element.43), kind=kCustom, calls=%fused_computation | custom fusion | bytes 139264 | tf_op jit(solution)/shard_map/jit(_take)/gather | solution.py:170
  55.6 5.0 %all-to-all-start.2 = ((f32[8,8,2048]{2,1,0:T(8,128)}), f32[8,8,2048]{2,1,0:T(8,128)S(1)}, u32[]{:S(2)}, u32[]{:S(2)}) async-start(f32[8,8,2048]{2,1,0:T(8,128)} %broadcast_in_dim.39), calls=%async_computation.2 | async-start | bytes 1048576 | tf_op jit(solution)/shard_map/all_to_all | solution.py:36
  61.9 7.6 %all-to-all-done.2 = f32[8,8,2048]{2,1,0:T(8,128)S(1)} async-done(((f32[8,8,2048]{2,1,0:T(8,128)}), f32[8,8,2048]{2,1,0:T(8,128)S(1)}, u32[]{:S(2)}, u32[]{:S(2)}) %all-to-all-start.2) | async-done | bytes 524320 | tf_op jit(solution)/shard_map/all_to_all | solution.py:36
  69.5 4.9 %all-to-all-start = ((f32[4,2,8,16,128]{4,2,1,3,0:T(8,128)}), f32[4,2,8,16,128]{4,2,1,3,0:T(8,128)S(1)}, u32[]{:S(2)}, u32[]{:S(2)}) async-start(f32[4,2,8,16,128]{4,2,1,3,0:T(8,128)} %copy.65), calls=%async_computation | async-start | bytes 1048576 | tf_op jit(solution)/shard_map/all_to_all | solution.py:60
  74.4 1.9 %collective-permute-start.4 = (f32[64,2048]{1,0:T(8,128)S(1)}, f32[64,2048]{1,0:T(8,128)S(1)}, u32[]{:S(2)}, u32[]{:S(2)}) collective-permute-start(f32[64,2048]{1,0:T(8,128)S(1)} %bitcast.147), channel_id=1, source_target_pairs={{0,1},{1,2},{2,3},{3,4},{4,5},{5,6},{6,7},{7,8},{8,9},{9,10},{10,1... | collective-permute-start | bytes 1572872 | tf_op jit(solution)/shard_map/ppermute | solution.py:25
  76.3 6.5 %collective-permute-start.5 = (f32[64,2048]{1,0:T(8,128)S(1)}, f32[64,2048]{1,0:T(8,128)S(1)}, u32[]{:S(2)}, u32[]{:S(2)}) collective-permute-start(f32[64,2048]{1,0:T(8,128)S(1)} %bitcast.148), channel_id=1, source_target_pairs={{1,0},{2,1},{3,2},{4,3},{5,4},{6,5},{7,6},{8,7},{9,8},{10,9},{11,1... | collective-permute-start | bytes 1572872 | tf_op jit(solution)/shard_map/ppermute | solution.py:27
  82.9 2.2 %copy.73 = f32[4,6144]{0,1:T(8,128)} copy(f32[4,6144]{1,0:T(4,128)S(1)} %pad_maximum_fusion.13) | data formatting | bytes 196608 | tf_op jit(solution)/shard_map/concatenate | solution.py:23
  85.1 4.2 %all_to_all.15 = f32[4,2,8,16,128]{4,2,0,3,1:T(8,128)S(1)} all-to-all(f32[4,2,8,16,128]{4,2,0,3,1:T(8,128)S(1)} %copy.66), channel_id=1, replica_groups=mesh['mem_0'=4,'mem_1'=2,'space'=64] {'mem_1'}, dimensions={1} | all-to-all | bytes 1048576 | tf_op jit(solution)/shard_map/all_to_all | solution.py:60
  90.5 1.4 copy.71
  92.2 1.3 copy.70
  93.5 1.3 copy.72
  94.8 3.7 %pad_maximum_fusion = f32[68,6144]{0,1:T(8,128)S(1)} fusion(f32[4,6144]{0,1:T(8,128)} %copy.73, f32[64,2048]{0,1:T(8,128)} %copy.72, f32[64,2048]{0,1:T(8,128)} %copy.71, f32[64,2048]{0,1:T(8,128)} %copy.70), kind=kLoop, calls=%fused_computation.2 | loop fusion | flops 1253376 | bytes 3342336 | tf_op jit(solution)/shard_map/concatenate | solution.py:184
  98.5 14.1 %gather_fusion.1 = f32[4096,68]{1,0:T(8,128)} fusion(f32[68,6144]{0,1:T(8,128)S(1)} %pad_maximum_fusion, s32[4096]{0:T(1024)S(1)} %broadcast_clamp_fusion), kind=kCustom, calls=%fused_computation.1 | custom fusion | bytes 2244608 | tf_op jit(solution)/shard_map/jit(_take)/gather | solution.py:185
  112.6 2.1 %copy.74 = f32[16,256,68]{1,2,0:T(8,128)S(1)} copy(f32[16,256,68]{2,1,0:T(8,128)} %bitcast.145) | data formatting | bytes 2228224 | tf_op jit(solution)/shard_map/jit(_take)/gather | solution.py:185
  115.6 1.3 multiply_reduce_fusion
  135.0 1.2 fusion.8
  (101 shorter events, 33.4 us)
Async XLA Ops:
  0.0 28.0 %copy-start.5 = (s32[2048]{0:T(1024)S(1)}, s32[2048]{0:T(1024)}, u32[]{:S(2)}) copy-start(s32[2048]{0:T(1024)} %param.15) | copy-start | bytes 24580
  0.0 27.9 %copy-start.3 = (f32[16,1024]{1,0:T(8,128)S(1)}, f32[16,1024]{1,0:T(8,128)}, u32[]{:S(2)}) copy-start(f32[16,1024]{1,0:T(8,128)} %param.11) | copy-start | bytes 196612
  0.0 27.9 %copy-start.2 = (f32[16,1024]{1,0:T(8,128)S(1)}, f32[16,1024]{1,0:T(8,128)}, u32[]{:S(2)}) copy-start(f32[16,1024]{1,0:T(8,128)} %param.12) | copy-start | bytes 196612
  0.0 34.1 %copy-start.1 = (f32[16,1024]{1,0:T(8,128)S(1)}, f32[16,1024]{1,0:T(8,128)}, u32[]{:S(2)}) copy-start(f32[16,1024]{1,0:T(8,128)} %param.13) | copy-start | bytes 196612
  0.0 28.0 %copy-start.4 = (s32[16,1,256]{2,1,0:T(1,128)S(1)}, s32[16,1,256]{2,1,0:T(1,128)}, u32[]{:S(2)}) copy-start(s32[16,1,256]{2,1,0:T(1,128)} %param.18) | copy-start | bytes 49156
  1.6 81.2 %collective-permute-start.6 = (f32[4,2048]{1,0:T(4,128)S(1)}, f32[4,2048]{1,0:T(4,128)S(1)}, u32[]{:S(2)}, u32[]{:S(2)}) collective-permute-start(f32[4,2048]{1,0:T(4,128)S(1)} %pad_maximum_fusion.18), channel_id=1, source_target_pairs={{0,1},{1,2},{2,3},{3,4},{4,5},{5,6},{6,7},{7,8},{8,9},{9,10},{10,1... | collective-permute-start | bytes 98312 | tf_op jit(solution)/shard_map/ppermute | solution.py:25
  5.4 77.4 %collective-permute-start.7 = (f32[4,2048]{1,0:T(4,128)S(1)}, f32[4,2048]{1,0:T(4,128)S(1)}, u32[]{:S(2)}, u32[]{:S(2)}) collective-permute-start(f32[4,2048]{1,0:T(4,128)S(1)} %pad_maximum_fusion.18), channel_id=1, source_target_pairs={{1,0},{2,1},{3,2},{4,3},{5,4},{6,5},{7,6},{8,7},{9,8},{10,9},{11,1... | collective-permute-start | bytes 98312 | tf_op jit(solution)/shard_map/ppermute | solution.py:27
  16.9 11.2 %collective-permute-start = (f32[4,4,1024]{2,1,0:T(4,128)S(1)}, f32[4,4,1024]{2,1,0:T(4,128)S(1)}, u32[]{:S(2)}, u32[]{:S(2)}) collective-permute-start(f32[4,4,1024]{2,1,0:T(4,128)S(1)} %get-tuple-element.37), channel_id=1, source_target_pairs={{0,1},{1,2},{2,3},{3,4},{4,5},{5,6},{6,7},{7,8},{8,9},{9,10},{10,1... | collective-permute-start | bytes 196616 | tf_op jit(solution)/shard_map/ppermute | solution.py:25
  18.8 15.3 %collective-permute-start.1 = (f32[4,4,1024]{2,1,0:T(4,128)S(1)}, f32[4,4,1024]{2,1,0:T(4,128)S(1)}, u32[]{:S(2)}, u32[]{:S(2)}) collective-permute-start(f32[4,4,1024]{2,1,0:T(4,128)S(1)} %get-tuple-element.38), channel_id=1, source_target_pairs={{1,0},{2,1},{3,2},{4,3},{5,4},{6,5},{7,6},{8,7},{9,8},{10,9},{11,1... | collective-permute-start | bytes 196616 | tf_op jit(solution)/shard_map/ppermute | solution.py:27
  26.0 9.0 %collective-permute-start.2 = (f32[8,4,1024]{2,1,0:T(4,128)S(1)}, f32[8,4,1024]{2,1,0:T(4,128)S(1)}, u32[]{:S(2)}, u32[]{:S(2)}) collective-permute-start(f32[8,4,1024]{2,1,0:T(4,128)S(1)} %get-tuple-element.23), channel_id=1, source_target_pairs={{0,1},{1,2},{2,3},{3,4},{4,5},{5,6},{6,7},{7,8},{8,9},{9,10},{10,1... | collective-permute-start | bytes 393224 | tf_op jit(solution)/shard_map/ppermute | solution.py:25
  28.1 8.5 %collective-permute-start.3 = (f32[8,4,1024]{2,1,0:T(4,128)S(1)}, f32[8,4,1024]{2,1,0:T(4,128)S(1)}, u32[]{:S(2)}, u32[]{:S(2)}) collective-permute-start(f32[8,4,1024]{2,1,0:T(4,128)S(1)} %get-tuple-element.24), channel_id=1, source_target_pairs={{1,0},{2,1},{3,2},{4,3},{5,4},{6,5},{7,6},{8,7},{9,8},{10,9},{11,1... | collective-permute-start | bytes 393224 | tf_op jit(solution)/shard_map/ppermute | solution.py:27
  55.6 27.2 %copy-start.6 = (f32[2048]{0:T(1024)S(1)}, f32[2048]{0:T(1024)}, u32[]{:S(2)}) copy-start(f32[2048]{0:T(1024)} %param.17) | copy-start | bytes 24580
  55.6 27.2 %copy-start.7 = (f32[2048]{0:T(1024)S(1)}, f32[2048]{0:T(1024)}, u32[]{:S(2)}) copy-start(f32[2048]{0:T(1024)} %param.16) | copy-start | bytes 24580
  55.6 13.9 %all-to-all-start.2 = ((f32[8,8,2048]{2,1,0:T(8,128)}), f32[8,8,2048]{2,1,0:T(8,128)S(1)}, u32[]{:S(2)}, u32[]{:S(2)}) async-start(f32[8,8,2048]{2,1,0:T(8,128)} %broadcast_in_dim.39), calls=%async_computation.2 | async-start | bytes 1048576 | tf_op jit(solution)/shard_map/all_to_all | solution.py:36
  69.5 15.6 %all-to-all-start = ((f32[4,2,8,16,128]{4,2,1,3,0:T(8,128)}), f32[4,2,8,16,128]{4,2,1,3,0:T(8,128)S(1)}, u32[]{:S(2)}, u32[]{:S(2)}) async-start(f32[4,2,8,16,128]{4,2,1,3,0:T(8,128)} %copy.65), calls=%async_computation | async-start | bytes 1048576 | tf_op jit(solution)/shard_map/all_to_all | solution.py:60
  74.4 17.8 %collective-permute-start.4 = (f32[64,2048]{1,0:T(8,128)S(1)}, f32[64,2048]{1,0:T(8,128)S(1)}, u32[]{:S(2)}, u32[]{:S(2)}) collective-permute-start(f32[64,2048]{1,0:T(8,128)S(1)} %bitcast.147), channel_id=1, source_target_pairs={{0,1},{1,2},{2,3},{3,4},{4,5},{5,6},{6,7},{7,8},{8,9},{9,10},{10,1... | collective-permute-start | bytes 1572872 | tf_op jit(solution)/shard_map/ppermute | solution.py:25
  76.3 17.2 %collective-permute-start.5 = (f32[64,2048]{1,0:T(8,128)S(1)}, f32[64,2048]{1,0:T(8,128)S(1)}, u32[]{:S(2)}, u32[]{:S(2)}) collective-permute-start(f32[64,2048]{1,0:T(8,128)S(1)} %bitcast.148), channel_id=1, source_target_pairs={{1,0},{2,1},{3,2},{4,3},{5,4},{6,5},{7,6},{8,7},{9,8},{10,9},{11,1... | collective-permute-start | bytes 1572872 | tf_op jit(solution)/shard_map/ppermute | solution.py:27
  114.7 0.7 copy-start.8
  131.9 3.2 %copy-start = (f32[64,16,128]{2,1,0:T(8,128)S(1)}, f32[64,16,128]{2,1,0:T(8,128)}, u32[]{:S(2)}) copy-start(f32[64,16,128]{2,1,0:T(8,128)} %bitcast_subtract_fusion) | copy-start | bytes 1572868
where the time goes:
time: 138 us; the launch traced here: 137 us
  starting transfers between devices  47.8 us (35%)
  local copies, waits for them, and re-layouts  41.7 us (30%)
  matrix products  20.5 us (15%)
  other arithmetic  12.4 us (9%)
  waiting for transfers between devices  10.2 us (7%)
  blocking collectives  4.15 us (3%)
    ppermute x4, starting transfers between devices, with_halo(): lax.ppermute(head, axis, [((i + 1) % count, i) for i in range(ends)])  28.3 us
    gather x2, local copies, waits for them, and re-layouts, body(): selected = jnp.take(combined, chosen, axis=1)  16.2 us
    ppermute x4, starting transfers between devices, with_halo(): lax.ppermute(tail, axis, [(i, (i + 1) % count) for i in range(ends)])  9.58 us
    gather x1, local copies, waits for them, and re-layouts, body(): readings = jnp.take(flattened, sensor_cell, axis=1)  8.84 us
    all_to_all x1, waiting for transfers between devices, copy_for_each(): return lax.all_to_all(copies, axis, split_axis=0, concat_axis=0, tiled=True)  7.6 us
    dot_general x8, matrix products, analyse(): jnp.matmul(inverse_root, iterate, precision=highest)  5.42 us
    dot_general x8, matrix products, analyse(): inverse_root = jnp.matmul(factor, inverse_root, precision=highest)  5.08 us
    all_to_all x1, starting transfers between devices, copy_for_each(): return lax.all_to_all(copies, axis, split_axis=0, concat_axis=0, tiled=True)  5.05 us
  transfers between devices with their start and end apart: 10, of which 4 were waited for; matrix products, arithmetic and copies ran while one was open for 21% of the time, Pallas kernels for 0%

commit v1 on v0

v1 whole, which is shorter than its diff:
```python
import functools

import jax
import jax.numpy as jnp
from jax import lax
from jax.experimental import pallas as pl
from jax.experimental.pallas import tpu as pltpu
from jax.sharding import PartitionSpec as P

TW = 128
STEPS = 4
NSITER = 8
RLOC = 8
EDGE = 16
MESH = pl.DeviceIdType.MESH
VMEM = pltpu.VMEM
f32 = jnp.float32
bf16 = jnp.bfloat16
i32 = jnp.int32


def split(x):
    high = x.astype(bf16)
    return high, (x - high.astype(f32)).astype(bf16)


def dot_nt(a, b):
    return lax.dot_general(a, b, (((1,), (1,)), ((), ())), preferred_element_type=f32)


def dot_nn(a, b):
    return jnp.dot(a, b, preferred_element_type=f32)


def gaspari(ratio):
    capped = jnp.maximum(ratio, 1.0)
    inner = (((-0.25 * ratio + 0.5) * ratio + 0.625) * ratio - 5.0 / 3.0) * ratio * ratio + 1.0
    outer = (
        ((((ratio / 12.0 - 0.5) * ratio + 0.625) * ratio + 5.0 / 3.0) * ratio - 5.0) * ratio
        + 4.0
        - 2.0 / (3.0 * capped)
    )
    return jnp.where(ratio <= 1.0, inner, jnp.where(ratio <= 2.0, outer, 0.0))


def forecast_kernel(
    strips, groups,
    members, flow_east, flow_north, mixing, land, lists,
    window, lists_prev, lists_next,
    buf0, buf1, coef, outbox,
    halo_send, halo_recv, mem_send, mem_recv, own_sem,
):
    s = lax.axis_index("space")
    m = lax.axis_index("mem")
    nxt = lax.rem(s + 1, strips)
    prv = lax.rem(s + strips - 1, strips)
    rows = members.shape[1]
    width = members.shape[2]
    barrier = pltpu.get_barrier_semaphore()
    for other in (prv, nxt):
        pl.semaphore_signal(barrier, inc=1, device_id={"space": other}, device_id_type=MESH)
    for step in range(1, groups):
        peer = lax.rem(m + step, groups)
        pl.semaphore_signal(barrier, inc=1, device_id={"mem": peer}, device_id_type=MESH)

    def fill(r):
        ocean = land[pl.ds(r, 1), :].astype(f32)
        coef[3 + r, 0:1, :] = 0.5 * flow_east[pl.ds(r, 1), :]
        coef[3 + r, 1:2, :] = 0.5 * flow_north[pl.ds(r, 1), :]
        coef[3 + r, 2:3, :] = mixing[pl.ds(r, 1), :]
        coef[3 + r, 3:4, :] = ocean
        buf0[STEPS + r] = members[:, r, :] * ocean

    for r in range(STEPS):
        fill(r)
    for r in range(rows - STEPS, rows):
        fill(r)
    pl.semaphore_wait(barrier, 2 + groups - 1)

    def to(k, src, dst, other):
        return pltpu.make_async_remote_copy(
            src_ref=src, dst_ref=dst, send_sem=halo_send.at[k], recv_sem=halo_recv.at[k],
            device_id={"space": other}, device_id_type=MESH,
        )

    last = STEPS + rows
    halo = [
        to(0, buf0.at[pl.ds(rows, STEPS)], buf0.at[pl.ds(0, STEPS)], nxt),
        to(1, buf0.at[pl.ds(STEPS, STEPS)], buf0.at[pl.ds(last, STEPS)], prv),
        to(2, coef.at[pl.ds(rows, 3)], coef.at[pl.ds(0, 3)], nxt),
        to(3, coef.at[pl.ds(3, 3)], coef.at[pl.ds(3 + rows, 3)], prv),
        to(4, lists, lists_prev, nxt),
        to(5, lists, lists_next, prv),
    ]
    for copy in halo:
        copy.start()
    for r in range(STEPS, rows - STEPS):
        fill(r)
    for copy in halo:
        copy.wait_recv()

    @pl.when(s == 0)
    def _():
        buf0[pl.ds(0, STEPS)] = jnp.zeros((STEPS, 8, width), f32)
        coef[pl.ds(0, 3)] = jnp.zeros((3, 4, width), f32)
        lists_prev[...] = jnp.full(lists_prev.shape, -(1 << 20), i32)

    @pl.when(s == strips - 1)
    def _():
        buf0[pl.ds(last, STEPS)] = jnp.zeros((STEPS, 8, width), f32)
        coef[pl.ds(3 + rows, 3)] = jnp.zeros((3, 4, width), f32)
        lists_next[...] = jnp.full(lists_next.shape, -(1 << 20), i32)

    for copy in halo:
        copy.wait_send()

    def advance(src, i):
        c = src[i]
        n = src[i + 1]
        so = src[i - 1]
        e = pltpu.roll(c, width - 1, 1)
        w = pltpu.roll(c, 1, 1)
        fe = coef[i - 1, 0:1, :]
        fn = coef[i - 1, 1:2, :]
        mx = coef[i - 1, 2:3, :]
        oc = coef[i - 1, 3:4, :]
        carried = fe * (e - w) + fn * (n - so)
        spread = e + w + n + so - 4.0 * c
        return oc * (c - carried + mx * spread)

    bufs = (buf0, buf1)
    for step in range(STEPS - 1):
        src, dst = bufs[step % 2], bufs[(step + 1) % 2]

        def one(i, _, src=src, dst=dst):
            dst[i] = advance(src, i)
            return 0

        lax.fori_loop(step + 1, 2 * STEPS + rows - 1 - step, one, 0)
    src = bufs[(STEPS - 1) % 2]
    lane = lax.broadcasted_iota(i32, (8, TW), 1)

    def final(g, _):
        packed = [jnp.zeros((8, TW), f32) for _ in range(groups)]
        for q in range(4):
            r = 4 * g + q
            value = advance(src, STEPS + r)
            blocks = [value[:, b * TW : (b + 1) * TW] for b in range(groups)]
            for b in range(groups):
                outbox[b, r] = blocks[b]
                both = jnp.where(lane < EDGE, blocks[(b + 1) % groups], blocks[(b - 1) % groups])
                turned = pltpu.roll(both, (32 * q + EDGE) % TW, 1)
                packed[b] = jnp.where(lane // 32 == q, turned, packed[b])
        for b in range(groups):
            outbox[b, rows + g] = packed[b]
        return 0

    lax.fori_loop(0, rows // 4, final, 0)
    mine = window.at[:, pl.ds(pl.multiple_of(8 * m, 8), 8), :]
    copies = []
    for k, step in enumerate((4, 3, 5, 2, 6, 7, 1)):
        peer = lax.rem(m + step, groups)
        copy = pltpu.make_async_remote_copy(
            src_ref=outbox.at[peer], dst_ref=mine, send_sem=mem_send.at[k], recv_sem=mem_recv.at[k],
            device_id={"mem": peer}, device_id_type=MESH,
        )
        copy.start()
        copies.append(copy)
    own = pltpu.make_async_copy(outbox.at[m], mine, own_sem)
    own.start()
    own.wait()
    for copy in copies:
        copy.wait()


def forecast(members, flow_east, flow_north, mixing, land, lists, strips, groups):
    rows, width = members.shape[1:]
    packed_rows = rows + rows // 4
    return pl.pallas_call(
        functools.partial(forecast_kernel, strips, groups),
        name="forecast",
        out_shape=[
            jax.ShapeDtypeStruct((packed_rows, 8 * groups, TW), f32),
            jax.ShapeDtypeStruct(lists.shape, i32),
            jax.ShapeDtypeStruct(lists.shape, i32),
        ],
        in_specs=[pl.BlockSpec(memory_space=VMEM)] * 6,
        out_specs=[pl.BlockSpec(memory_space=VMEM)] * 3,
        scratch_shapes=[
            VMEM((rows + 2 * STEPS, 8, width), f32),
            VMEM((rows + 2 * STEPS, 8, width), f32),
            VMEM((rows + 6, 4, width), f32),
            VMEM((groups, packed_rows, 8, TW), f32),
            pltpu.SemaphoreType.DMA((6,)),
            pltpu.SemaphoreType.DMA((6,)),
            pltpu.SemaphoreType.DMA((groups - 1,)),
            pltpu.SemaphoreType.DMA((groups - 1,)),
            pltpu.SemaphoreType.DMA,
        ],
        compiler_params=pltpu.CompilerParams(
            collective_id=0, has_side_effects=True, vmem_limit_bytes=60 * 1024 * 1024
        ),
    )(members, flow_east, flow_north, mixing, land, lists)


def weight_kernel(
    width, per_strip, block_ref, lists_prev, lists, lists_next, cells, values, noises,
    weight, forced, place_ref, row_ref, w_ref, u_ref,
):
    chunks = per_strip // TW
    rows = lists.shape[0]
    block = block_ref[0]
    start = block * TW
    middle = start.astype(f32) + (TW - 1) / 2.0
    lane_rows = lax.broadcasted_iota(i32, (8, TW), 0)
    for d, source in enumerate((lists_prev, lists, lists_next)):
        for half in range(rows // 8):
            for side in range(lists.shape[1] // TW):
                entry = source[8 * half : 8 * half + 8, side * TW : (side + 1) * TW]
                j = entry + (d - 2) * per_strip
                usable = (j >= 0) & (j < per_strip)
                j = jnp.where(usable, j, 0)
                low = j & (TW - 1)
                high = j >> 7
                cell = jnp.zeros((8, TW), i32)
                value = jnp.zeros((8, TW), f32)
                noise = jnp.ones((8, TW), f32)
                for c in range(chunks):
                    here = high == c

                    def pick(table, c=c, low=low):
                        full = jnp.broadcast_to(table[c : c + 1, :], (8, TW))
                        return jnp.take_along_axis(full, low, axis=1, mode="promise_in_bounds")

                    cell = jnp.where(here, pick(cells), cell)
                    value = jnp.where(here, pick(values), value)
                    noise = jnp.where(here, pick(noises), noise)
                row = cell // width
                col = cell % width
                tile_row = lane_rows + (8 * half + (d - 1) * rows)
                dy = (row - tile_row).astype(f32)
                a = jnp.abs(col.astype(f32) - middle)
                a = jnp.minimum(a, float(width) - a)
                dx = jnp.maximum(a - (TW - 1) / 2.0, 0.0)
                distance = jnp.sqrt(dx * dx + dy * dy)
                w = jnp.where(usable, gaspari(distance / RLOC) / noise, 0.0)
                p = (col - start) & (width - 1)
                edge = jnp.where(p < TW + EDGE, p - TW + EDGE, p - (width - EDGE))
                edge = TW + 32 * (row & 3) + edge
                near = (p < TW + EDGE) | (p >= width - EDGE)
                place = jnp.where(p < TW, p, jnp.where(near, edge, -1))
                at = (pl.ds(rows * d + 8 * half, 8), pl.ds(side * TW, TW))
                place_ref[at] = place
                row_ref[at] = row
                w_ref[at] = w
                u_ref[at] = w * value

    slots = lists.shape[1]
    cell_iota = lax.broadcasted_iota(i32, (2 * TW, slots), 0)
    row_iota = lax.broadcasted_iota(i32, (rows, slots), 0)
    quad_iota = lax.broadcasted_iota(i32, (4, slots), 0)

    def one(t, _):
        place = place_ref[pl.ds(t, 1), :]
        row = row_ref[pl.ds(t, 1), :]
        w = w_ref[pl.ds(t, 1), :]
        u = u_ref[pl.ds(t, 1), :]
        hot = jnp.where(cell_iota == place, 1.0, 0.0).astype(bf16)
        parts = []
        for x in (w, u):
            high = x.astype(bf16).astype(f32)
            parts += [high, x - high]
        main = [jnp.where(row_iota == row, x, 0.0) for x in parts]
        quad = [jnp.where(quad_iota == row // 4, x, 0.0) for x in parts]
        both = jnp.concatenate(quad, axis=0)
        lhs = jnp.concatenate(main + [both], axis=0).astype(bf16)
        out = dot_nt(lhs, hot)
        weight[t, 0:rows, :] = out[0:rows, :TW] + out[rows : 2 * rows, :TW]
        forced[t, 0:rows, :] = out[2 * rows : 3 * rows, :TW] + out[3 * rows : 4 * rows, :TW]
        e = out[4 * rows :, TW:]
        weight[t, rows : rows + 4, :] = e[0:4] + e[4:8]
        forced[t, rows : rows + 4, :] = e[8:12] + e[12:16]
        return 0

    lax.fori_loop(0, 3 * rows, one, 0, unroll=4)


def weights(block, lists_prev, lists, lists_next, cells, values, noises, width):
    rows, slots = lists.shape
    per_strip = cells.shape[0]
    packed_rows = rows + rows // 4
    tables = [x.reshape(per_strip // TW, TW) for x in (cells, values, noises)]
    return pl.pallas_call(
        functools.partial(weight_kernel, width, per_strip),
        name="weights",
        out_shape=[jax.ShapeDtypeStruct((3 * rows, packed_rows, TW), f32)] * 2,
        in_specs=[pl.BlockSpec(memory_space=pltpu.SMEM)] + [pl.BlockSpec(memory_space=VMEM)] * 6,
        out_specs=[pl.BlockSpec(memory_space=VMEM)] * 2,
        scratch_shapes=[
            VMEM((3 * rows, slots), i32),
            VMEM((3 * rows, slots), i32),
            VMEM((3 * rows, slots), f32),
            VMEM((3 * rows, slots), f32),
        ],
        compiler_params=pltpu.CompilerParams(vmem_limit_bytes=60 * 1024 * 1024),
    )(block, lists_prev, lists, lists_next, *tables)


def gram_kernel(rows, window, weight, forced, gram, forcing, centred, hilo, dref):
    packed_rows, count, _ = window.shape
    tiles = packed_rows // 2
    for i in range(packed_rows):
        x = window[i]
        mean = jnp.sum(x, axis=0, keepdims=True) / count
        x = x - mean
        centred[i] = x
        at = pl.ds((i % 2) * TW, TW)
        high, low = split(x)
        hilo[i // 2, 0:count, at] = high
        hilo[i // 2, count : 2 * count, at] = low
        dref[:, i * TW : (i + 1) * TW] = forced[:, i, :] - weight[:, i, :] * mean
    total = jnp.zeros((2 * 3 * rows, 2 * count), f32)
    for k in range(tiles):
        high, low = split(dref[:, k * 2 * TW : (k + 1) * 2 * TW])
        total += dot_nt(jnp.concatenate([high, low], axis=0), hilo[k])
    total = total[: 3 * rows] + total[3 * rows :]
    forcing[...] = total + pltpu.roll(total, count, 1)

    def tile(t, need):
        acc = None
        for k in need:
            x = jnp.concatenate([centred[2 * k], centred[2 * k + 1]], axis=1)
            w = jnp.concatenate(
                [weight[t, 2 * k : 2 * k + 1, :], weight[t, 2 * k + 1 : 2 * k + 2, :]], axis=1
            )
            high, low = split(x * w)
            part = dot_nt(jnp.concatenate([high, low], axis=0), hilo[k])
            acc = part if acc is None else acc + part
        acc = acc[:count] + acc[count:]
        return acc + pltpu.roll(acc, count, 1)

    left = lax.broadcasted_iota(i32, (count, 2 * count), 1) < count
    main = rows // 2
    quarter = rows // 4

    for j in range(4):
        need = {
            1: tuple(range(tiles)),
            2: tuple(range(2 * j, main)) + ((main, main + 1) if j < 2 else (main + 1,)),
            0: tuple(range(0, 2 * j + 2)) + ((main,) if j < 2 else (main, main + 1)),
        }

        def pair(h, _, j=j, need=need):
            r = quarter * j + 2 * h
            for d in (0, 2, 1):
                a = tile(rows * d + r, need[d])
                b = tile(rows * d + r + 1, need[d])
                gram[4 * d + j, :, pl.ds(pl.multiple_of(h * 2 * count, 2 * count), 2 * count)] = jnp.where(left, a, b)
            return 0

        lax.fori_loop(0, 2, pair, 0)


def grams(window, weight, forced, rows):
    packed_rows, count, _ = window.shape
    return pl.pallas_call(
        functools.partial(gram_kernel, rows),
        name="grams",
        out_shape=[
            jax.ShapeDtypeStruct((12, count, 4 * count), f32),
            jax.ShapeDtypeStruct((3 * rows, 2 * count), f32),
        ],
        in_specs=[pl.BlockSpec(memory_space=VMEM)] * 3,
        out_specs=[pl.BlockSpec(memory_space=VMEM)] * 2,
        scratch_shapes=[
            VMEM((packed_rows, count, TW), f32),
            VMEM((packed_rows // 2, 2 * count, 2 * TW), bf16),
            VMEM((3 * rows, packed_rows * TW), f32),
        ],
        compiler_params=pltpu.CompilerParams(vmem_limit_bytes=60 * 1024 * 1024),
    )(window, weight, forced)


def share_kernel(strips, rows, gram, forcing, total, force, got_g, got_f, send, recv):
    s = lax.axis_index("space")
    nxt = lax.rem(s + 1, strips)
    prv = lax.rem(s + strips - 1, strips)
    barrier = pltpu.get_barrier_semaphore()
    for other in (prv, nxt):
        pl.semaphore_signal(barrier, inc=1, device_id={"space": other}, device_id_type=MESH)
    pl.semaphore_wait(barrier, 2)

    def to(k, src, dst, other):
        return pltpu.make_async_remote_copy(
            src_ref=src, dst_ref=dst, send_sem=send.at[k], recv_sem=recv.at[k],
            device_id={"space": other}, device_id_type=MESH,
        )

    copies = [
        to(0, gram.at[pl.ds(8, 4)], got_g.at[0], nxt),
        to(1, gram.at[pl.ds(0, 4)], got_g.at[1], prv),
        to(2, forcing.at[pl.ds(2 * rows, rows)], got_f.at[0], nxt),
        to(3, forcing.at[pl.ds(0, rows)], got_f.at[1], prv),
    ]
    for copy in copies:
        copy.start()
    total[...] = gram[pl.ds(4, 4)]
    force[...] = forcing[pl.ds(rows, rows)]
    for copy in copies:
        copy.wait()

    @pl.when(s > 0)
    def _():
        total[...] += got_g[0]
        force[...] += got_f[0]

    @pl.when(s < strips - 1)
    def _():
        total[...] += got_g[1]
        force[...] += got_f[1]


def share(gram, forcing, strips, rows):
    _, count, lanes = gram.shape
    return pl.pallas_call(
        functools.partial(share_kernel, strips, rows),
        name="share",
        out_shape=[
            jax.ShapeDtypeStruct((4, count, lanes), f32),
            jax.ShapeDtypeStruct((rows, forcing.shape[1]), f32),
        ],
        in_specs=[pl.BlockSpec(memory_space=VMEM)] * 2,
        out_specs=[pl.BlockSpec(memory_space=VMEM)] * 2,
        scratch_shapes=[
            VMEM((2, 4, count, lanes), f32),
            VMEM((2, rows, forcing.shape[1]), f32),
            pltpu.SemaphoreType.DMA((4,)),
            pltpu.SemaphoreType.DMA((4,)),
        ],
        compiler_params=pltpu.CompilerParams(collective_id=1, has_side_effects=True),
    )(gram, forcing)


def analysis_kernel(rows, gram, force, window, out):
    count = gram.shape[1]
    lanes = gram.shape[2]
    per = lanes // count
    row_of = lax.broadcasted_iota(i32, (count, lanes), 0)
    lane_of = lax.broadcasted_iota(i32, (count, lanes), 1)
    eye = jnp.where(row_of == lane_of % count, 1.0, 0.0).astype(f32)
    seg_row = lax.broadcasted_iota(i32, (lanes, lanes), 0) // count
    seg_col = lax.broadcasted_iota(i32, (lanes, lanes), 1) // count
    diag = seg_row == seg_col
    diag_one = jnp.where(diag, 1.0, 0.0).astype(bf16)

    def blocked(x):
        zero = jnp.zeros((), bf16)
        return jnp.where(diag, jnp.concatenate([x] * per, axis=0), zero)

    def parts(x):
        high, low = split(x)
        return (high, low), (blocked(high), blocked(low))

    def mul(a, b):
        (ah, al), (bh, bl) = a, b
        return dot_nn(ah, bh) + dot_nn(al, bh) + dot_nn(ah, bl)

    quads = rows // per
    z, r, scale = [], [], []
    for g in range(quads):
        b = eye + gram[g] / (count - 1)
        sq = jnp.sum(b * b, axis=0, keepdims=True)
        h1 = sq.astype(bf16)
        rest = sq - h1.astype(f32)
        h2 = rest.astype(bf16)
        h3 = (rest - h2.astype(f32)).astype(bf16)
        stacked = jnp.concatenate([jnp.broadcast_to(h, (16, lanes)) for h in (h1, h2, h3)], axis=0)
        sums = dot_nn(stacked, diag_one)
        frob = jnp.sqrt(sums[0:1] + sums[16:17] + sums[32:33])
        z.append(b / frob)
        scale.append(jnp.sqrt(frob))
    for step in range(NSITER):
        for g in range(quads):
            zl, zr = parts(z[g])
            if step == 0:
                f = 1.5 * eye - 0.5 * z[g]
                fl, _ = parts(f)
                r.append(f)
                z[g] = mul(fl, zr)
                continue
            rl, rr = parts(r[g])
            f = 1.5 * eye - 0.5 * mul(rl, zr)
            fl, _ = parts(f)
            if step < NSITER - 1:
                z[g] = mul(fl, zr)
            r[g] = mul(fl, rr)
    low_half = lax.broadcasted_iota(i32, (count, 2 * count), 1) < count
    for g in range(quads):
        t = r[g] / scale[g]
        (th, tl), tr = parts(t)
        vec = jnp.broadcast_to(force[g : g + 1, :], (16, lanes))
        vec = mul(split(vec), tr)
        vec = mul(split(vec), tr) / (count - 1)
        mix = t + vec[0:1]
        for h in range(per // 2):
            two = mix[:, h * 2 * count : (h + 1) * 2 * count]
            row0 = per * g + 2 * h
            fields, means = [], []
            for q in range(2):
                x = window[row0 + q]
                mean = jnp.sum(x, axis=0, keepdims=True) / count
                fields.append(x - mean)
                means.append(mean)
            xh, xl = split(jnp.concatenate(fields, axis=0))
            for q in range(2):
                keep = low_half if q == 0 else jnp.logical_not(low_half)
                lh, ll = split(jnp.where(keep, two, 0.0))
                out[:, row0 + q, :] = means[q] + (dot_nn(lh, xh) + dot_nn(ll, xh) + dot_nn(lh, xl))


def analyse(gram, force, window, rows):
    count = gram.shape[1]
    return pl.pallas_call(
        functools.partial(analysis_kernel, rows),
        name="analysis",
        out_shape=jax.ShapeDtypeStruct((count, rows, TW), f32),
        in_specs=[pl.BlockSpec(memory_space=VMEM)] * 3,
        out_specs=pl.BlockSpec(memory_space=VMEM),
        compiler_params=pltpu.CompilerParams(vmem_limit_bytes=60 * 1024 * 1024),
    )(gram, force, window)


def body(strips, groups, members, flow_east, flow_north, mixing, land_mask, sensor_cell,
         sensor_value, sensor_noise, tile_lists, tile_counts):
    rows, width = members.shape[1:]
    slot = jnp.arange(tile_lists.shape[2], dtype=i32)
    lists = jnp.where(slot[None, :] < tile_counts, tile_lists[:, 0, :], -(1 << 20))
    block = lax.axis_index("mem").astype(i32).reshape(1)
    window, lists_prev, lists_next = forecast(
        members, flow_east, flow_north, mixing, land_mask, lists, strips, groups
    )
    weight, forced = weights(
        block, lists_prev, lists, lists_next, sensor_cell, sensor_value, sensor_noise, width
    )
    gram, forcing = grams(window, weight, forced, rows)
    total, force = share(gram, forcing, strips, rows)
    count = window.shape[1]
    force = force[:, :count].reshape(rows // 4, 4 * count)
    return analyse(total, force, window, rows)


def solution(mesh):
    strips, groups = mesh.shape["space"], mesh.shape["mem"]
    in_specs = (
        P("mem", "space", None),
        P("space", None),
        P("space", None),
        P("space", None),
        P("space", None),
        P("space"),
        P("space"),
        P("space"),
        P("space", "mem", None),
        P("space", "mem"),
    )
    return jax.shard_map(
        functools.partial(body, strips, groups),
        mesh=mesh,
        in_specs=in_specs,
        out_specs=P(None, "space", "mem"),
        check_vma=False,
    )
```

time: 138 us -> 86.4 us (0.63)
  the two profiles are of different devices: /device:TPU:14 before, /device:TPU:1 now
where the time goes in v1:
time: 86.4 us; the launch traced here: 86 us
  Pallas kernels  83.2 us (96%)
  local copies, waits for them, and re-layouts  2.08 us (2%)
    pallas_call x1, Pallas kernels, forecast(): pl.pallas_call(functools.partial(forecast_kernel, strips, groups), name='...  38.9 us
    pallas_call x1, Pallas kernels, share(): pl.pallas_call(functools.partial(share_kernel, strips, rows), name='share...  13.4 us
    pallas_call x1, Pallas kernels, analyse(): pl.pallas_call(functools.partial(analysis_kernel, rows), name='analysis',...  13.2 us
    pallas_call x1, Pallas kernels, grams(): pl.pallas_call(functools.partial(gram_kernel, rows), name='grams', out_sh...  11.5 us
    pallas_call x1, Pallas kernels, weights(): pl.pallas_call(functools.partial(weight_kernel, width, per_strip), name='...  6.22 us

profile of v1, /device:TPU:1, one launch (start us, length us, event | category | flops | bytes accessed | tf_op | source)
XLA Modules:
  0.0 86.0 jit_solution(6336916260494370573)
XLA Ops:
  0.0 0.0 copy-start
  0.0 0.0 copy-start.1
  0.0 0.7 copy-done
  0.7 0.0 copy-done.1
  0.7 0.7 bitcast_select_fusion.lists
  1.4 38.9 %forecast.1 = (f32[20,64,128]{2,1,0:T(8,128)}, s32[16,256]{1,0:T(8,128)}, s32[16,256]{1,0:T(8,128)}) custom-call(f32[8,16,1024]{2,1,0:T(8,128)} %members.1, f32[16,1024]{1,0:T(8,128)} %flow_east.1, f32[16,1024]{1,0:T(8,128)} %flow_north.1, f32[16,1024]{1,0:T(8,128)} %mixing.1, s32[16,1024]{1,0:T(8,128)} %land.1, s32[16,256]{1,0:T(8,128)} %bitcast_select_fusion.lists), custom_call_target="tpu_custom_call" | custom-call | tf_op jit(solution)/shard_map/forecast/pallas_call | solution.py:179
  40.3 6.2 %weights.1 = (f32[48,20,128]{2,1,0:T(8,128)}, f32[48,20,128]{2,1,0:T(8,128)}) custom-call(s32[1]{0:T(128)} %bitcast.1.block_ref, s32[16,256]{1,0:T(8,128)} %get-tuple-element.15.lists_prev, s32[16,256]{1,0:T(8,128)} %bitcast_select_fusion.lists, s32[16,256]{1,0:T(8,128)} %get-tuple-element.16.lists_next, s32[16,128]{1,0:T(8,128)} %bitcast.8, ...), custom_call_target="tpu_custom_call" | custom-call | tf_op jit(solution)/shard_map/weights/pallas_call | solution.py:293
  46.5 11.5 %grams.1 = (f32[12,64,256]{2,1,0:T(8,128)}, f32[48,128]{1,0:T(8,128)}) custom-call(f32[20,64,128]{2,1,0:T(8,128)} %get-tuple-element.14.window, f32[48,20,128]{2,1,0:T(8,128)} %get-tuple-element.17.weight, f32[48,20,128]{2,1,0:T(8,128)} %get-tuple-element.18.forced), custom_call_target="tpu_custom_call" | custom-call | tf_op jit(solution)/shard_map/grams/pallas_call | solution.py:366
  58.0 13.4 %share.1 = (f32[4,64,256]{2,1,0:T(8,128)}, f32[16,128]{1,0:T(8,128)}) custom-call(f32[12,64,256]{2,1,0:T(8,128)} %get-tuple-element.19.gram, f32[48,128]{1,0:T(8,128)} %get-tuple-element.20.forcing), custom_call_target="tpu_custom_call" | custom-call | tf_op jit(solution)/shard_map/share/pallas_call | solution.py:425
  71.5 1.4 %reshape.19.force = f32[4,256]{1,0:T(4,128)} reshape(f32[16,64]{1,0:T(8,128)} %bitcast.11) | data formatting | bytes 8192 | tf_op jit(solution)/shard_map/reshape | solution.py:548
  72.8 13.2 %analysis.1 = f32[64,16,128]{2,1,0:T(8,128)} custom-call(f32[4,64,256]{2,1,0:T(8,128)} %get-tuple-element.21.gram, f32[4,256]{1,0:T(4,128)} %reshape.19.force, f32[20,64,128]{2,1,0:T(8,128)} %get-tuple-element.14.window), custom_call_target="tpu_custom_call" | custom-call | tf_op jit(solution)/shard_map/analysis/pallas_call | solution.py:523
Async XLA Ops:
  0.0 0.7 copy-start
  0.0 0.7 copy-start.1

commit v2 on v1

v2 whole, which is shorter than its diff:
```python
import functools

import jax
import jax.numpy as jnp
from jax import lax
from jax.experimental import pallas as pl
from jax.experimental.pallas import tpu as pltpu
from jax.sharding import PartitionSpec as P

TW = 128
STEPS = 4
NSITER = 8
RLOC = 8
EDGE = 16
MESH = pl.DeviceIdType.MESH
VMEM = pltpu.VMEM
f32 = jnp.float32
bf16 = jnp.bfloat16
i32 = jnp.int32


def split(x):
    high = x.astype(bf16)
    return high, (x - high.astype(f32)).astype(bf16)


def dot_nt(a, b):
    return lax.dot_general(a, b, (((1,), (1,)), ((), ())), preferred_element_type=f32)


def dot_nn(a, b):
    return jnp.dot(a, b, preferred_element_type=f32)


def gaspari(ratio):
    capped = jnp.maximum(ratio, 1.0)
    inner = (((-0.25 * ratio + 0.5) * ratio + 0.625) * ratio - 5.0 / 3.0) * ratio * ratio + 1.0
    outer = (
        ((((ratio / 12.0 - 0.5) * ratio + 0.625) * ratio + 5.0 / 3.0) * ratio - 5.0) * ratio
        + 4.0
        - 2.0 / (3.0 * capped)
    )
    return jnp.where(ratio <= 1.0, inner, jnp.where(ratio <= 2.0, outer, 0.0))


def cycle_kernel(
    strips, groups,
    members, flow_east, flow_north, mixing, land, tile_lists, tile_counts, cells, values, noises,
    window, total,
    buf0, buf1, coef, outbox, lists, place_ref, row_ref, w_ref, u_ref,
    weight, forced, centred, means, hilo, to_next, to_prev, got,
    halo_send, halo_recv, mem_send, mem_recv, own_sem,
    next_send, next_recv, prev_send, prev_recv,
):
    s = lax.axis_index("space")
    m = lax.axis_index("mem")
    nxt = lax.rem(s + 1, strips)
    prv = lax.rem(s + strips - 1, strips)
    rows = members.shape[1]
    width = members.shape[2]
    slots = tile_lists.shape[2]
    chunks = cells.shape[0]
    per_strip = chunks * TW
    count = 8 * groups
    barrier = pltpu.get_barrier_semaphore()
    for other in (prv, nxt):
        pl.semaphore_signal(barrier, inc=1, device_id={"space": other}, device_id_type=MESH)
    for step in range(1, groups):
        peer = lax.rem(m + step, groups)
        pl.semaphore_signal(barrier, inc=1, device_id={"mem": peer}, device_id_type=MESH)

    def fill(r):
        ocean = land[pl.ds(r, 1), :].astype(f32)
        coef[3 + r, 0:1, :] = 0.5 * flow_east[pl.ds(r, 1), :]
        coef[3 + r, 1:2, :] = 0.5 * flow_north[pl.ds(r, 1), :]
        coef[3 + r, 2:3, :] = mixing[pl.ds(r, 1), :]
        coef[3 + r, 3:4, :] = ocean
        buf0[STEPS + r] = members[:, r, :] * ocean

    for r in range(STEPS):
        fill(r)
    for r in range(rows - STEPS, rows):
        fill(r)
    slot = lax.broadcasted_iota(i32, (rows, slots), 1)
    lists[pl.ds(rows, rows)] = jnp.where(slot < tile_counts[...], tile_lists[:, 0, :], -(1 << 20))
    pl.semaphore_wait(barrier, 2 + groups - 1)

    def to(k, src, dst, other, send=halo_send, recv=halo_recv):
        return pltpu.make_async_remote_copy(
            src_ref=src, dst_ref=dst, send_sem=send.at[k], recv_sem=recv.at[k],
            device_id={"space": other}, device_id_type=MESH,
        )

    last = STEPS + rows
    mine_l = lists.at[pl.ds(rows, rows)]
    halo = [
        to(0, buf0.at[pl.ds(rows, STEPS)], buf0.at[pl.ds(0, STEPS)], nxt),
        to(1, buf0.at[pl.ds(STEPS, STEPS)], buf0.at[pl.ds(last, STEPS)], prv),
        to(2, coef.at[pl.ds(rows, 3)], coef.at[pl.ds(0, 3)], nxt),
        to(3, coef.at[pl.ds(3, 3)], coef.at[pl.ds(3 + rows, 3)], prv),
        to(4, mine_l, lists.at[pl.ds(0, rows)], nxt),
        to(5, mine_l, lists.at[pl.ds(2 * rows, rows)], prv),
    ]
    for copy in halo:
        copy.start()
    for r in range(STEPS, rows - STEPS):
        fill(r)

    start = m * TW
    middle = start.astype(f32) + (TW - 1) / 2.0
    lane_rows = lax.broadcasted_iota(i32, (8, TW), 0)

    def attributes(d):
        for half in range(rows // 8):
            for side in range(slots // TW):
                at = (pl.ds(pl.multiple_of(rows * d + 8 * half, 8), 8), pl.ds(side * TW, TW))
                j = lists[at] + (d - 2) * per_strip
                usable = (j >= 0) & (j < per_strip)
                j = jnp.where(usable, j, 0)
                low = j & (TW - 1)
                high = j >> 7
                cell = jnp.zeros((8, TW), i32)
                value = jnp.zeros((8, TW), f32)
                noise = jnp.ones((8, TW), f32)
                for c in range(chunks):
                    here = high == c

                    def pick(table, c=c, low=low):
                        full = jnp.broadcast_to(table[c : c + 1, :], (8, TW))
                        return jnp.take_along_axis(full, low, axis=1, mode="promise_in_bounds")

                    cell = jnp.where(here, pick(cells), cell)
                    value = jnp.where(here, pick(values), value)
                    noise = jnp.where(here, pick(noises), noise)
                shift = width.bit_length() - 1
                row = cell >> shift
                col = cell & (width - 1)
                tile_row = lane_rows + (8 * half + (d - 1) * rows)
                dy = (row - tile_row).astype(f32)
                a = jnp.abs(col.astype(f32) - middle)
                a = jnp.minimum(a, float(width) - a)
                dx = jnp.maximum(a - (TW - 1) / 2.0, 0.0)
                distance = jnp.sqrt(dx * dx + dy * dy)
                w = jnp.where(usable, gaspari(distance / RLOC) / noise, 0.0)
                p = (col - start) & (width - 1)
                edge = jnp.where(p < TW + EDGE, p - TW + EDGE, p - (width - EDGE))
                edge = TW + 32 * (row & 3) + edge
                near = (p < TW + EDGE) | (p >= width - EDGE)
                place_ref[at] = jnp.where(p < TW, p, jnp.where(near, edge, -1))
                row_ref[at] = row
                w_ref[at] = w
                u_ref[at] = w * value

    half = rows // 2
    cell_iota = lax.broadcasted_iota(i32, (2 * TW, slots), 0)
    ri = lax.broadcasted_iota(i32, (rows, slots), 0)
    row_iota = 2 * (ri & (half - 1)) + ri // half
    qi = lax.broadcasted_iota(i32, (4, slots), 0)
    quad_iota = 2 * (qi & 1) + (qi >> 1)

    def scatter(t):
        place = place_ref[pl.ds(t, 1), :]
        row = row_ref[pl.ds(t, 1), :]
        hot = jnp.where(cell_iota == place, 1.0, 0.0).astype(bf16)
        parts = []
        for x in (w_ref[pl.ds(t, 1), :], u_ref[pl.ds(t, 1), :]):
            high = x.astype(bf16).astype(f32)
            parts += [high, x - high]
        main = [jnp.where(row_iota == row, x, 0.0) for x in parts]
        quad = [jnp.where(quad_iota == (row >> 2), x, 0.0) for x in parts]
        both = jnp.concatenate(quad, axis=0)
        lhs = jnp.concatenate(main + [both], axis=0).astype(bf16)
        out = dot_nt(lhs, hot)
        for k, ref in ((0, weight), (2, forced)):
            x = out[k * rows : (k + 1) * rows, :TW] + out[(k + 1) * rows : (k + 2) * rows, :TW]
            ref[t, 0:half, 0:TW] = x[0:half]
            ref[t, 0:half, TW : 2 * TW] = x[half:rows]
            at = 4 * rows + 4 * k
            e = out[at : at + 4, TW:] + out[at + 4 : at + 8, TW:]
            ref[t, half : half + 2, 0:TW] = e[0:2]
            ref[t, half : half + 2, TW : 2 * TW] = e[2:4]

    attributes(jnp.int32(1))

    def scatter_own(i, _):
        for q in range(4):
            scatter(rows + 4 * i + q)
        return 0

    lax.fori_loop(0, rows // 4, scatter_own, 0)

    for copy in halo:
        copy.wait_recv()

    @pl.when(s == 0)
    def _():
        buf0[pl.ds(0, STEPS)] = jnp.zeros((STEPS, 8, width), f32)
        coef[pl.ds(0, 3)] = jnp.zeros((3, 4, width), f32)
        lists[pl.ds(0, rows)] = jnp.full((rows, slots), -(1 << 20), i32)

    @pl.when(s == strips - 1)
    def _():
        buf0[pl.ds(last, STEPS)] = jnp.zeros((STEPS, 8, width), f32)
        coef[pl.ds(3 + rows, 3)] = jnp.zeros((3, 4, width), f32)
        lists[pl.ds(2 * rows, rows)] = jnp.full((rows, slots), -(1 << 20), i32)

    for copy in halo:
        copy.wait_send()

    def advance(src, i):
        c = src[i]
        n = src[i + 1]
        so = src[i - 1]
        e = pltpu.roll(c, width - 1, 1)
        w = pltpu.roll(c, 1, 1)
        fe = coef[i - 1, 0:1, :]
        fn = coef[i - 1, 1:2, :]
        mx = coef[i - 1, 2:3, :]
        oc = coef[i - 1, 3:4, :]
        carried = fe * (e - w) + fn * (n - so)
        spread = e + w + n + so - 4.0 * c
        return oc * (c - carried + mx * spread)

    bufs = (buf0, buf1)
    for step in range(STEPS - 1):
        src, dst = bufs[step % 2], bufs[(step + 1) % 2]

        def one(i, _, src=src, dst=dst):
            dst[i] = advance(src, i)
            return 0

        lax.fori_loop(step + 1, 2 * STEPS + rows - 1 - step, one, 0)
    src = bufs[(STEPS - 1) % 2]
    lane = lax.broadcasted_iota(i32, (8, TW), 1)

    def final(g, _):
        packed = [jnp.zeros((8, TW), f32) for _ in range(groups)]
        for q in range(4):
            r = 4 * g + q
            value = advance(src, STEPS + r)
            blocks = [value[:, b * TW : (b + 1) * TW] for b in range(groups)]
            for b in range(groups):
                outbox[b, r] = blocks[b]
                both = jnp.where(lane < EDGE, blocks[(b + 1) % groups], blocks[(b - 1) % groups])
                turned = pltpu.roll(both, (32 * q + EDGE) % TW, 1)
                packed[b] = jnp.where(lane // 32 == q, turned, packed[b])
        for b in range(groups):
            outbox[b, rows + g] = packed[b]
        return 0

    lax.fori_loop(0, rows // 4, final, 0)
    mine = window.at[:, pl.ds(pl.multiple_of(8 * m, 8), 8), :]
    copies = []
    for k, step in enumerate((4, 3, 5, 2, 6, 7, 1)):
        peer = lax.rem(m + step, groups)
        copy = pltpu.make_async_remote_copy(
            src_ref=outbox.at[peer], dst_ref=mine, send_sem=mem_send.at[k], recv_sem=mem_recv.at[k],
            device_id={"mem": peer}, device_id_type=MESH,
        )
        copy.start()
        copies.append(copy)
    own = pltpu.make_async_copy(outbox.at[m], mine, own_sem)
    own.start()

    def attributes_far(i, _):
        attributes(2 * i)
        return 0

    lax.fori_loop(0, 2, attributes_far, 0)

    def scatter_far(i, _):
        for q in range(4):
            scatter(jnp.where(i < rows // 4, 4 * i, 4 * i + rows) + q)
        return 0

    lax.fori_loop(0, rows // 2, scatter_far, 0)
    own.wait()
    for copy in copies:
        copy.wait()

    packed_rows = window.shape[0]
    tiles = packed_rows // 2

    def centre(k, _):
        x = jnp.concatenate([window[2 * k], window[2 * k + 1]], axis=1)
        mean = jnp.sum(x, axis=0, keepdims=True) * (1.0 / count)
        x = x - mean
        centred[k] = x
        means[pl.ds(k, 1), :] = mean
        high, low = split(x)
        both = jnp.concatenate([high, low], axis=0)
        zero = jnp.zeros((2 * count, 2 * TW), bf16)
        hilo[k, 0, 0 : 2 * count, :] = both
        hilo[k, 0, 2 * count : 4 * count, :] = zero
        hilo[k, 1, 0 : 2 * count, :] = zero
        hilo[k, 1, 2 * count : 4 * count, :] = both
        return 0

    lax.fori_loop(0, tiles, centre, 0)

    def left(k, base, factor=None):
        x = centred[k]
        mean = means[pl.ds(k, 1), :]
        pieces, vectors = [], []
        for q in range(4):
            w = weight[base + q, pl.ds(k, 1), :]
            u = forced[base + q, pl.ds(k, 1), :]
            if factor is not None:
                w = w * factor
                u = u * factor
            high, low = split(x * w)
            pieces += [high, low]
            vectors.append(u - w * mean)
        v = jnp.concatenate(vectors + [jnp.zeros((4, 2 * TW), f32)], axis=0)
        top = v.astype(bf16).astype(f32)
        pieces.append(jnp.concatenate([top, v - top], axis=0).astype(bf16))
        return jnp.concatenate(pieces, axis=0)

    low_half = lax.broadcasted_iota(i32, (count, TW), 1) < count
    low_row = lax.broadcasted_iota(i32, (1, TW), 1) < count

    def store(ref, at, acc):
        folded = []
        for q in range(4):
            x = acc[2 * q * count : (2 * q + 1) * count] + acc[(2 * q + 1) * count : (2 * q + 2) * count]
            folded.append(x + pltpu.roll(x, count, 1))
        v = acc[8 * count : 8 * count + 8] + acc[8 * count + 8 : 8 * count + 16]
        v = v + pltpu.roll(v, count, 1)
        for h in range(2):
            lanes = slice(h * TW, (h + 1) * TW)
            ref[at, 0:count, lanes] = jnp.where(low_half, folded[2 * h], folded[2 * h + 1])
            row = jnp.where(low_row, v[2 * h : 2 * h + 1], v[2 * h + 1 : 2 * h + 2])
            ref[at, count : count + 8, lanes] = jnp.broadcast_to(row, (8, TW))

    main = rows // 2

    def ahead_copy(c):
        return to(c, to_next.at[c], got.at[0, c], nxt, next_send, next_recv)

    def behind_copy(c):
        return to(c, to_prev.at[c + 1], got.at[1, c], prv, prev_send, prev_recv)

    def far(c, _):
        nb = 2 * rows + 4 * c
        pb = 4 * (c - 1)
        acc = None

        def add(acc, k, base, sel, factor=None):
            part = dot_nt(left(k, base, factor), hilo[k, sel])
            return part if acc is None else acc + part

        for k in range(main):
            ahead = 2 * c <= k
            acc = add(acc, k, jnp.where(ahead, nb, pb), jnp.where(ahead, 0, 1))
        ahead = c < 4
        acc = add(acc, main + 1, jnp.where(ahead, nb, pb), jnp.where(ahead, 0, 1))
        behind = c >= 1
        acc = add(acc, main, jnp.where(behind, pb, nb), jnp.where(behind, 1, 0))
        factor = jnp.where((c == 1) | (c == 3), jnp.float32(1.0), jnp.float32(0.0))
        base = jnp.where(c == 1, nb, jnp.where(c == 3, pb, 0))
        acc = add(acc, jnp.where(c == 3, main + 1, main), base, jnp.where(c == 3, 1, 0), factor)
        store(to_next, c, acc[:, 0:TW])
        store(to_prev, c, acc[:, TW : 2 * TW])

        @pl.when(c < 4)
        def _():
            ahead_copy(c).start()

        @pl.when(c >= 1)
        def _():
            behind_copy(c - 1).start()

        return 0

    lax.fori_loop(0, 5, far, 0)

    def near(j, _):
        acc = None
        for k in range(tiles):
            part = dot_nt(left(k, rows + 4 * j), hilo[k, 0, 0 : 2 * count, :])
            acc = part if acc is None else acc + part
        store(total, j, acc)
        return 0

    lax.fori_loop(0, 4, near, 0)
    for c in range(4):
        ahead_copy(c).wait()
        behind_copy(c).wait()

    @pl.when(s > 0)
    def _():
        total[...] += got[0]

    @pl.when(s < strips - 1)
    def _():
        total[...] += got[1]


def cycle(members, flow_east, flow_north, mixing, land, lists, counts, cells, values, noises, strips, groups):
    rows, width = members.shape[1:]
    slots = lists.shape[2]
    packed_rows = rows + rows // 4
    tiles = packed_rows // 2
    count = 8 * groups
    tables = [x.reshape(-1, TW) for x in (cells, values, noises)]
    dma = pltpu.SemaphoreType.DMA
    return pl.pallas_call(
        functools.partial(cycle_kernel, strips, groups),
        name="cycle",
        out_shape=[
            jax.ShapeDtypeStruct((packed_rows, count, TW), f32),
            jax.ShapeDtypeStruct((4, count + 8, 4 * count), f32),
        ],
        in_specs=[pl.BlockSpec(memory_space=VMEM)] * 10,
        out_specs=[pl.BlockSpec(memory_space=VMEM)] * 2,
        scratch_shapes=[
            VMEM((rows + 2 * STEPS, 8, width), f32),
            VMEM((rows + 2 * STEPS, 8, width), f32),
            VMEM((rows + 6, 4, width), f32),
            VMEM((groups, packed_rows, 8, TW), f32),
            VMEM((3 * rows, slots), i32),
            VMEM((3 * rows, slots), i32),
            VMEM((3 * rows, slots), i32),
            VMEM((3 * rows, slots), f32),
            VMEM((3 * rows, slots), f32),
            VMEM((3 * rows, tiles, 2 * TW), f32),
            VMEM((3 * rows, tiles, 2 * TW), f32),
            VMEM((tiles, count, 2 * TW), f32),
            VMEM((tiles, 2 * TW), f32),
            VMEM((tiles, 2, 4 * count, 2 * TW), bf16),
            VMEM((5, count + 8, 4 * count), f32),
            VMEM((5, count + 8, 4 * count), f32),
            VMEM((2, 4, count + 8, 4 * count), f32),
            dma((6,)), dma((6,)), dma((groups - 1,)), dma((groups - 1,)), dma,
            dma((4,)), dma((4,)), dma((4,)), dma((4,)),
        ],
        compiler_params=pltpu.CompilerParams(
            collective_id=0, has_side_effects=True, vmem_limit_bytes=40 * 1024 * 1024
        ),
    )(members, flow_east, flow_north, mixing, land, lists, counts, *tables)


def analysis_kernel(gram, window, out, zs, rs, scales):
    quads, count, lanes = zs.shape
    per = lanes // count
    row_of = lax.broadcasted_iota(i32, (count, lanes), 0)
    lane_of = lax.broadcasted_iota(i32, (count, lanes), 1)
    eye = jnp.where(row_of == lane_of % count, 1.0, 0.0).astype(f32)
    seg_row = lax.broadcasted_iota(i32, (lanes, lanes), 0) // count
    seg_col = lax.broadcasted_iota(i32, (lanes, lanes), 1) // count
    diag = seg_row == seg_col
    diag_one = jnp.where(diag, 1.0, 0.0).astype(bf16)

    def blocked(x):
        return jnp.where(diag, jnp.concatenate([x] * per, axis=0), jnp.zeros((), bf16))

    def right(x):
        return blocked(x[0]), blocked(x[1])

    def mul(a, b):
        (ah, al), (bh, bl) = a, b
        n = ah.shape[0]
        p = dot_nn(jnp.concatenate([ah, al], axis=0), bh)
        return p[:n] + p[n:] + dot_nn(ah, bl)

    for g in range(quads):
        b = eye + gram[g, 0:count, :] / (count - 1)
        sq = jnp.sum(b * b, axis=0, keepdims=True)
        h1 = sq.astype(bf16)
        rest = sq - h1.astype(f32)
        h2 = rest.astype(bf16)
        h3 = (rest - h2.astype(f32)).astype(bf16)
        stacked = jnp.concatenate([jnp.broadcast_to(h, (16, lanes)) for h in (h1, h2, h3)], axis=0)
        sums = dot_nn(stacked, diag_one)
        frob = jnp.sqrt(sums[0:1] + sums[16:17] + sums[32:33])
        z = b / frob
        scales[pl.ds(g, 1), :] = jnp.sqrt(frob)
        f = 1.5 * eye - 0.5 * z
        rs[g] = f
        zs[g] = mul(split(f), right(split(z)))

    def step(i, _):
        for g in range(quads):
            r, zr = split(rs[g]), right(split(zs[g]))
            f = split(1.5 * eye - 0.5 * mul(r, zr))
            zs[g] = mul(f, zr)
            rs[g] = mul(f, right(r))
        return 0

    lax.fori_loop(0, NSITER - 2, step, 0)
    low_half = lax.broadcasted_iota(i32, (count, 2 * count), 1) < count

    for g in range(quads):
        r = split(rs[g])
        f = split(1.5 * eye - 0.5 * mul(r, right(split(zs[g]))))
        t = mul(f, right(r)) / scales[pl.ds(g, 1), :]
        tr = right(split(t))
        vec = jnp.broadcast_to(gram[g, count : count + 1, :], (16, lanes))
        vec = mul(split(vec), tr)
        vec = mul(split(vec), tr) / (count - 1)
        mix = t + vec[0:1]
        for h in range(per // 2):
            two = mix[:, h * 2 * count : (h + 1) * 2 * count]
            row0 = per * g + 2 * h
            fields, averages = [], []
            for q in range(2):
                x = window[row0 + q]
                mean = jnp.sum(x, axis=0, keepdims=True) * (1.0 / count)
                fields.append(x - mean)
                averages.append(mean)
            x = split(jnp.concatenate(fields, axis=0))
            lhs = jnp.concatenate([jnp.where(low_half, two, 0.0), jnp.where(low_half, 0.0, two)], axis=0)
            y = mul(split(lhs), x)
            for q in range(2):
                out[:, row0 + q, :] = averages[q] + y[q * count : (q + 1) * count]


def analyse(gram, window, rows):
    quads, _, lanes = gram.shape
    count = window.shape[1]
    return pl.pallas_call(
        analysis_kernel,
        name="analysis",
        out_shape=jax.ShapeDtypeStruct((count, rows, TW), f32),
        in_specs=[pl.BlockSpec(memory_space=VMEM)] * 2,
        out_specs=pl.BlockSpec(memory_space=VMEM),
        scratch_shapes=[
            VMEM((quads, count, lanes), f32),
            VMEM((quads, count, lanes), f32),
            VMEM((quads, lanes), f32),
        ],
        compiler_params=pltpu.CompilerParams(vmem_limit_bytes=16 * 1024 * 1024),
    )(gram, window)


def body(strips, groups, members, flow_east, flow_north, mixing, land_mask, sensor_cell,
         sensor_value, sensor_noise, tile_lists, tile_counts):
    window, total = cycle(
        members, flow_east, flow_north, mixing, land_mask, tile_lists, tile_counts,
        sensor_cell, sensor_value, sensor_noise, strips, groups,
    )
    return analyse(total, window, members.shape[1])


def solution(mesh):
    strips, groups = mesh.shape["space"], mesh.shape["mem"]
    in_specs = (
        P("mem", "space", None),
        P("space", None),
        P("space", None),
        P("space", None),
        P("space", None),
        P("space"),
        P("space"),
        P("space"),
        P("space", "mem", None),
        P("space", "mem"),
    )
    return jax.shard_map(
        functools.partial(body, strips, groups),
        mesh=mesh,
        in_specs=in_specs,
        out_specs=P(None, "space", "mem"),
        check_vma=False,
    )
```

time: 86.4 us -> 66.5 us (0.77)
  Pallas kernels: 83.2 us -> 58.7 us
  local copies, waits for them, and re-layouts: 2.08 us -> 7.26 us
    pallas_call x5 -> x2, Pallas kernels: 83.2 us -> 58.7 us  [the longest x1 47.3 us: cycle(): pl.pallas_call(functools.partial(cycle_kernel, strips, groups), name='cyc...]
    unnamed x4 -> x19, local copies, waits for them, and re-layouts: 0.72 us -> 7.26 us
    reshape x1 -> x0, local copies, waits for them, and re-layouts: 1.37 us -> none  [body(): force = force[:, :count].reshape(rows // 4, 4 * count)]
where the time goes in v2:
time: 66.5 us; the launch traced here: 66 us
  Pallas kernels  58.7 us (88%)
  local copies, waits for them, and re-layouts  7.26 us (11%)
    pallas_call x1, Pallas kernels, cycle(): pl.pallas_call(functools.partial(cycle_kernel, strips, groups), name='cyc...  47.3 us
    pallas_call x1, Pallas kernels, analyse(): pl.pallas_call(analysis_kernel, name='analysis', out_shape=jax.ShapeDtype...  11.4 us
    unnamed x19, local copies, waits for them, and re-layouts  7.26 us

profile of v2, /device:TPU:1, one launch (start us, length us, event | category | flops | bytes accessed | tf_op | source)
XLA Modules:
  0.0 66.0 jit_solution(15692318342075367244)
XLA Ops:
  0.0 0.0 copy-start.6
  0.0 0.7 %copy.11.tile_counts = s32[16,1]{1,0:T(8,128)S(1)} copy(s32[16,1]{0,1:T(1,128)} %param.19) | data formatting | bytes 128 | tf_op args[9]
  0.7 0.0 copy-done.6
  0.8 0.0 copy-start
  0.8 1.0 %copy-done = f32[8,16,1024]{2,1,0:T(8,128)S(1)} copy-done((f32[8,16,1024]{2,1,0:T(8,128)S(1)}, f32[8,16,1024]{2,1,0:T(8,128)}, u32[]{:S(2)}) %copy-start) | copy-done | bytes 524312
  1.8 0.0 copy-start.1
  1.8 0.8 %copy-done.1 = f32[16,1024]{1,0:T(8,128)S(1)} copy-done((f32[16,1024]{1,0:T(8,128)S(1)}, f32[16,1024]{1,0:T(8,128)}, u32[]{:S(2)}) %copy-start.1) | copy-done | bytes 65560
  2.6 0.0 copy-start.2
  2.6 0.8 %copy-done.2 = f32[16,1024]{1,0:T(8,128)S(1)} copy-done((f32[16,1024]{1,0:T(8,128)S(1)}, f32[16,1024]{1,0:T(8,128)}, u32[]{:S(2)}) %copy-start.2) | copy-done | bytes 65560
  3.5 0.0 copy-start.3
  3.5 0.8 %copy-done.3 = f32[16,1024]{1,0:T(8,128)S(1)} copy-done((f32[16,1024]{1,0:T(8,128)S(1)}, f32[16,1024]{1,0:T(8,128)}, u32[]{:S(2)}) %copy-start.3) | copy-done | bytes 65560
  4.3 0.0 copy-start.4
  4.3 0.8 %copy-done.4 = s32[16,1024]{1,0:T(8,128)S(1)} copy-done((s32[16,1024]{1,0:T(8,128)S(1)}, s32[16,1024]{1,0:T(8,128)}, u32[]{:S(2)}) %copy-start.4) | copy-done | bytes 65560
  5.2 0.0 copy-start.5
  5.2 0.7 %copy-done.5 = s32[16,1,256]{2,1,0:T(1,128)S(1)} copy-done((s32[16,1,256]{2,1,0:T(1,128)S(1)}, s32[16,1,256]{2,1,0:T(1,128)}, u32[]{:S(2)}) %copy-start.5) | copy-done | bytes 16408
  5.9 0.0 copy-start.7
  5.9 0.7 %copy-done.7 = f32[2048]{0:T(1024)S(1)} copy-done((f32[2048]{0:T(1024)S(1)}, f32[2048]{0:T(1024)}, u32[]{:S(2)}) %copy-start.7) | copy-done | bytes 8216
  6.6 0.0 copy-start.8
  6.6 0.7 %copy-done.8 = f32[2048]{0:T(1024)S(1)} copy-done((f32[2048]{0:T(1024)S(1)}, f32[2048]{0:T(1024)}, u32[]{:S(2)}) %copy-start.8) | copy-done | bytes 8216
  7.3 47.3 %cycle.1 = (f32[20,64,128]{2,1,0:T(8,128)S(1)}, f32[4,72,256]{2,1,0:T(8,128)S(1)}) custom-call(f32[8,16,1024]{2,1,0:T(8,128)S(1)} %copy-done, f32[16,1024]{1,0:T(8,128)S(1)} %copy-done.1, f32[16,1024]{1,0:T(8,128)S(1)} %copy-done.2, f32[16,1024]{1,0:T(8,128)S(1)} %copy-done.3, s32[16,1024]{1,0:T(8,128)S(1)} %copy-done.4, s32[16,1,256]{2,1,0:T(1,128)S(1)} %copy-done.5, ...), custom_call_target="tpu_custom_call" | custom-call | tf_op jit(solution)/shard_map/cycle/pallas_call | solution.py:407
  54.6 11.4 %analysis.1 = f32[64,16,128]{2,1,0:T(8,128)} custom-call(f32[4,72,256]{2,1,0:T(8,128)S(1)} %get-tuple-element.7.gram, f32[20,64,128]{2,1,0:T(8,128)S(1)} %get-tuple-element.8.window), custom_call_target="tpu_custom_call" | custom-call | tf_op jit(solution)/shard_map/analysis/pallas_call | solution.py:521
Async XLA Ops:
  0.0 0.7 %copy-start.6 = (s32[2048]{0:T(1024)S(1)}, s32[2048]{0:T(1024)}, u32[]{:S(2)}) copy-start(s32[2048]{0:T(1024)} %param.15) | copy-start | bytes 24580
  0.8 1.0 %copy-start = (f32[8,16,1024]{2,1,0:T(8,128)S(1)}, f32[8,16,1024]{2,1,0:T(8,128)}, u32[]{:S(2)}) copy-start(f32[8,16,1024]{2,1,0:T(8,128)} %members.1) | copy-start | bytes 1572868
  1.8 0.8 %copy-start.1 = (f32[16,1024]{1,0:T(8,128)S(1)}, f32[16,1024]{1,0:T(8,128)}, u32[]{:S(2)}) copy-start(f32[16,1024]{1,0:T(8,128)} %flow_east.1) | copy-start | bytes 196612
  2.6 0.8 %copy-start.2 = (f32[16,1024]{1,0:T(8,128)S(1)}, f32[16,1024]{1,0:T(8,128)}, u32[]{:S(2)}) copy-start(f32[16,1024]{1,0:T(8,128)} %flow_north.1) | copy-start | bytes 196612
  3.5 0.8 %copy-start.3 = (f32[16,1024]{1,0:T(8,128)S(1)}, f32[16,1024]{1,0:T(8,128)}, u32[]{:S(2)}) copy-start(f32[16,1024]{1,0:T(8,128)} %mixing.1) | copy-start | bytes 196612
  4.3 0.8 %copy-start.4 = (s32[16,1024]{1,0:T(8,128)S(1)}, s32[16,1024]{1,0:T(8,128)}, u32[]{:S(2)}) copy-start(s32[16,1024]{1,0:T(8,128)} %land.1) | copy-start | bytes 196612
  5.2 0.7 %copy-start.5 = (s32[16,1,256]{2,1,0:T(1,128)S(1)}, s32[16,1,256]{2,1,0:T(1,128)}, u32[]{:S(2)}) copy-start(s32[16,1,256]{2,1,0:T(1,128)} %tile_lists.1) | copy-start | bytes 49156
  5.9 0.7 %copy-start.7 = (f32[2048]{0:T(1024)S(1)}, f32[2048]{0:T(1024)}, u32[]{:S(2)}) copy-start(f32[2048]{0:T(1024)} %param.16) | copy-start | bytes 24580
  6.6 0.7 %copy-start.8 = (f32[2048]{0:T(1024)S(1)}, f32[2048]{0:T(1024)}, u32[]{:S(2)}) copy-start(f32[2048]{0:T(1024)} %param.17) | copy-start | bytes 24580

commit v3 on v2

--- a/solution.py
+++ b/solution.py
@@ -45,13 +45,24 @@
 
 def cycle_kernel(
     strips, groups,
+    members_h, east_h, north_h, mixing_h, land_h, lists_h, counts_h, cells_h, values_h, noises_h,
+    centred, means, total,
     members, flow_east, flow_north, mixing, land, tile_lists, tile_counts, cells, values, noises,
-    window, total,
-    buf0, buf1, coef, outbox, lists, place_ref, row_ref, w_ref, u_ref,
-    weight, forced, centred, means, hilo, to_next, to_prev, got,
-    halo_send, halo_recv, mem_send, mem_recv, own_sem,
+    window, buf0, buf1, buf2, coef, outbox, lists, place_ref, row_ref, w_ref, u_ref,
+    weight, forced, hilo, to_next, to_prev, got,
+    load_sem, halo_send, halo_recv, mem_send, mem_recv, own_sem,
     next_send, next_recv, prev_send, prev_recv,
 ):
+    loads = [
+        pltpu.make_async_copy(src, dst, load_sem.at[k])
+        for k, (src, dst) in enumerate((
+            (members_h, members), (land_h, land), (east_h, flow_east), (north_h, flow_north),
+            (mixing_h, mixing), (lists_h, tile_lists), (cells_h, cells), (values_h, values),
+            (noises_h, noises), (counts_h, tile_counts),
+        ))
+    ]
+    for copy in loads:
+        copy.start()
     s = lax.axis_index("space")
     m = lax.axis_index("mem")
     nxt = lax.rem(s + 1, strips)
@@ -77,12 +88,17 @@
         coef[3 + r, 3:4, :] = ocean
         buf0[STEPS + r] = members[:, r, :] * ocean
 
+    for copy in loads:
+        copy.wait()
     for r in range(STEPS):
         fill(r)
     for r in range(rows - STEPS, rows):
         fill(r)
     slot = lax.broadcasted_iota(i32, (rows, slots), 1)
-    lists[pl.ds(rows, rows)] = jnp.where(slot < tile_counts[...], tile_lists[:, 0, :], -(1 << 20))
+    square = lax.broadcasted_iota(i32, (rows, rows), 0) == lax.broadcasted_iota(i32, (rows, rows), 1)
+    used = jnp.where(square, jnp.broadcast_to(tile_counts[...].astype(f32), (rows, rows)), 0.0)
+    used = jnp.sum(used, axis=1, keepdims=True)
+    lists[pl.ds(rows, rows)] = jnp.where(slot.astype(f32) < used, tile_lists[:, 0, :], -(1 << 20))
     pl.semaphore_wait(barrier, 2 + groups - 1)
 
     def to(k, src, dst, other, send=halo_send, recv=halo_recv):
@@ -173,12 +189,12 @@
         out = dot_nt(lhs, hot)
         for k, ref in ((0, weight), (2, forced)):
             x = out[k * rows : (k + 1) * rows, :TW] + out[(k + 1) * rows : (k + 2) * rows, :TW]
-            ref[t, 0:half, 0:TW] = x[0:half]
-            ref[t, 0:half, TW : 2 * TW] = x[half:rows]
             at = 4 * rows + 4 * k
             e = out[at : at + 4, TW:] + out[at + 4 : at + 8, TW:]
-            ref[t, half : half + 2, 0:TW] = e[0:2]
-            ref[t, half : half + 2, TW : 2 * TW] = e[2:4]
+            low, high = x[0:half], x[half:rows]
+            part = half // 2
+            ref[t, :, 0:TW] = jnp.concatenate([low[:part], e[0:1], low[part:], e[1:2]], axis=0)
+            ref[t, :, TW : 2 * TW] = jnp.concatenate([high[:part], e[2:3], high[part:], e[3:4]], axis=0)
 
     attributes(jnp.int32(1))
 
@@ -188,24 +204,6 @@
         return 0
 
     lax.fori_loop(0, rows // 4, scatter_own, 0)
-
-    for copy in halo:
-        copy.wait_recv()
-
-    @pl.when(s == 0)
-    def _():
-        buf0[pl.ds(0, STEPS)] = jnp.zeros((STEPS, 8, width), f32)
-        coef[pl.ds(0, 3)] = jnp.zeros((3, 4, width), f32)
-        lists[pl.ds(0, rows)] = jnp.full((rows, slots), -(1 << 20), i32)
-
-    @pl.when(s == strips - 1)
-    def _():
-        buf0[pl.ds(last, STEPS)] = jnp.zeros((STEPS, 8, width), f32)
-        coef[pl.ds(3 + rows, 3)] = jnp.zeros((3, 4, width), f32)
-        lists[pl.ds(2 * rows, rows)] = jnp.full((rows, slots), -(1 << 20), i32)
-
-    for copy in halo:
-        copy.wait_send()
 
     def advance(src, i):
         c = src[i]
@@ -221,46 +219,81 @@
         spread = e + w + n + so - 4.0 * c
         return oc * (c - carried + mx * spread)
 
-    bufs = (buf0, buf1)
+    chain = (buf0, buf1, buf2, buf1)
     for step in range(STEPS - 1):
-        src, dst = bufs[step % 2], bufs[(step + 1) % 2]
-
-        def one(i, _, src=src, dst=dst):
-            dst[i] = advance(src, i)
+        src, dst = chain[step], chain[step + 1]
+
+        def inner(i, _, src=src, dst=dst, first=STEPS + 1 + step):
+            for q in range(2):
+                dst[first + 2 * i + q] = advance(src, first + 2 * i + q)
             return 0
 
-        lax.fori_loop(step + 1, 2 * STEPS + rows - 1 - step, one, 0)
-    src = bufs[(STEPS - 1) % 2]
+        lax.fori_loop(0, (rows - 2 - 2 * step) // 2, inner, 0)
+
+    for copy in halo:
+        copy.wait_recv()
+
+    @pl.when(s == 0)
+    def _():
+        buf0[pl.ds(0, STEPS)] = jnp.zeros((STEPS, 8, width), f32)
+        coef[pl.ds(0, 3)] = jnp.zeros((3, 4, width), f32)
+        lists[pl.ds(0, rows)] = jnp.full((rows, slots), -(1 << 20), i32)
+
+    @pl.when(s == strips - 1)
+    def _():
+        buf0[pl.ds(last, STEPS)] = jnp.zeros((STEPS, 8, width), f32)
+        coef[pl.ds(3 + rows, 3)] = jnp.zeros((3, 4, width), f32)
+        lists[pl.ds(2 * rows, rows)] = jnp.full((rows, slots), -(1 << 20), i32)
+
+    for copy in halo:
+        copy.wait_send()
+
+    for step in range(STEPS - 1):
+        src, dst = chain[step], chain[step + 1]
+
+        def outer(i, _, src=src, dst=dst, low=step + 1, high=rows + STEPS - 1 - step):
+            dst[low + i] = advance(src, low + i)
+            dst[high + i] = advance(src, high + i)
+            return 0
+
+        lax.fori_loop(0, STEPS, outer, 0)
+    src = chain[STEPS - 1]
     lane = lax.broadcasted_iota(i32, (8, TW), 1)
 
-    def final(g, _):
+    packed_rows = window.shape[0]
+    chunk = packed_rows // 2
+
+    def final(g, _, shift=0):
         packed = [jnp.zeros((8, TW), f32) for _ in range(groups)]
         for q in range(4):
             r = 4 * g + q
             value = advance(src, STEPS + r)
             blocks = [value[:, b * TW : (b + 1) * TW] for b in range(groups)]
             for b in range(groups):
-                outbox[b, r] = blocks[b]
+                outbox[b, r + shift] = blocks[b]
                 both = jnp.where(lane < EDGE, blocks[(b + 1) % groups], blocks[(b - 1) % groups])
                 turned = pltpu.roll(both, (32 * q + EDGE) % TW, 1)
                 packed[b] = jnp.where(lane // 32 == q, turned, packed[b])
         for b in range(groups):
-            outbox[b, rows + g] = packed[b]
-        return 0
-
-    lax.fori_loop(0, rows // 4, final, 0)
-    mine = window.at[:, pl.ds(pl.multiple_of(8 * m, 8), 8), :]
-    copies = []
-    for k, step in enumerate((4, 3, 5, 2, 6, 7, 1)):
-        peer = lax.rem(m + step, groups)
-        copy = pltpu.make_async_remote_copy(
-            src_ref=outbox.at[peer], dst_ref=mine, send_sem=mem_send.at[k], recv_sem=mem_recv.at[k],
-            device_id={"mem": peer}, device_id_type=MESH,
-        )
-        copy.start()
-        copies.append(copy)
-    own = pltpu.make_async_copy(outbox.at[m], mine, own_sem)
-    own.start()
+            outbox[b, rows // 2 + 4 * shift + g] = packed[b]
+        return 0
+
+    copies, own = [], []
+    for part in range(2):
+        lax.fori_loop(2 * part, 2 * part + 2, functools.partial(final, shift=2 * part), 0)
+        here = pl.ds(chunk * part, chunk)
+        mine = window.at[here, pl.ds(pl.multiple_of(8 * m, 8), 8), :]
+        for k, step in enumerate((4, 3, 5, 2, 6, 7, 1)):
+            peer = lax.rem(m + step, groups)
+            at = part * (groups - 1) + k
+            copy = pltpu.make_async_remote_copy(
+                src_ref=outbox.at[peer, here], dst_ref=mine, send_sem=mem_send.at[at],
+                recv_sem=mem_recv.at[at], device_id={"mem": peer}, device_id_type=MESH,
+            )
+            copy.start()
+            copies.append(copy)
+        own.append(pltpu.make_async_copy(outbox.at[m, here], mine, own_sem.at[part]))
+        own[part].start()
 
     def attributes_far(i, _):
         attributes(2 * i)
@@ -274,11 +307,6 @@
         return 0
 
     lax.fori_loop(0, rows // 2, scatter_far, 0)
-    own.wait()
-    for copy in copies:
-        copy.wait()
-
-    packed_rows = window.shape[0]
     tiles = packed_rows // 2
 
     def centre(k, _):
@@ -287,16 +315,14 @@
         x = x - mean
         centred[k] = x
         means[pl.ds(k, 1), :] = mean
-        high, low = split(x)
-        both = jnp.concatenate([high, low], axis=0)
-        zero = jnp.zeros((2 * count, 2 * TW), bf16)
-        hilo[k, 0, 0 : 2 * count, :] = both
-        hilo[k, 0, 2 * count : 4 * count, :] = zero
-        hilo[k, 1, 0 : 2 * count, :] = zero
-        hilo[k, 1, 2 * count : 4 * count, :] = both
-        return 0
-
-    lax.fori_loop(0, tiles, centre, 0)
+        high = x.astype(bf16).astype(f32)
+        both = jnp.concatenate([high, x - high], axis=0).T.astype(bf16)
+        zero = jnp.zeros((2 * TW, 2 * count), bf16)
+        hilo[k, 0, :, 0 : 2 * count] = both
+        hilo[k, 0, :, 2 * count : 4 * count] = zero
+        hilo[k, 1, :, 0 : 2 * count] = zero
+        hilo[k, 1, :, 2 * count : 4 * count] = both
+        return 0
 
     def left(k, base, factor=None):
         x = centred[k]
@@ -319,7 +345,10 @@
     low_half = lax.broadcasted_iota(i32, (count, TW), 1) < count
     low_row = lax.broadcasted_iota(i32, (1, TW), 1) < count
 
-    def store(ref, at, acc):
+    def store(ref, at, acc, more=False):
+        def put(dst, value):
+            ref[dst] = ref[dst] + value if more else value
+
         folded = []
         for q in range(4):
             x = acc[2 * q * count : (2 * q + 1) * count] + acc[(2 * q + 1) * count : (2 * q + 2) * count]
@@ -328,11 +357,13 @@
         v = v + pltpu.roll(v, count, 1)
         for h in range(2):
             lanes = slice(h * TW, (h + 1) * TW)
-            ref[at, 0:count, lanes] = jnp.where(low_half, folded[2 * h], folded[2 * h + 1])
+            put((at, slice(0, count), lanes), jnp.where(low_half, folded[2 * h], folded[2 * h + 1]))
             row = jnp.where(low_row, v[2 * h : 2 * h + 1], v[2 * h + 1 : 2 * h + 2])
-            ref[at, count : count + 8, lanes] = jnp.broadcast_to(row, (8, TW))
+            put((at, slice(count, count + 8), lanes), jnp.broadcast_to(row, (8, TW)))
 
     main = rows // 2
+    part_k = main // 2
+    edge_a, edge_b = part_k, 2 * part_k + 1
 
     def ahead_copy(c):
         return to(c, to_next.at[c], got.at[0, c], nxt, next_send, next_recv)
@@ -346,19 +377,19 @@
         acc = None
 
         def add(acc, k, base, sel, factor=None):
-            part = dot_nt(left(k, base, factor), hilo[k, sel])
+            part = dot_nn(left(k, base, factor), hilo[k, sel])
             return part if acc is None else acc + part
 
         for k in range(main):
             ahead = 2 * c <= k
-            acc = add(acc, k, jnp.where(ahead, nb, pb), jnp.where(ahead, 0, 1))
+            acc = add(acc, k + k // part_k, jnp.where(ahead, nb, pb), jnp.where(ahead, 0, 1))
         ahead = c < 4
-        acc = add(acc, main + 1, jnp.where(ahead, nb, pb), jnp.where(ahead, 0, 1))
+        acc = add(acc, edge_b, jnp.where(ahead, nb, pb), jnp.where(ahead, 0, 1))
         behind = c >= 1
-        acc = add(acc, main, jnp.where(behind, pb, nb), jnp.where(behind, 1, 0))
+        acc = add(acc, edge_a, jnp.where(behind, pb, nb), jnp.where(behind, 1, 0))
         factor = jnp.where((c == 1) | (c == 3), jnp.float32(1.0), jnp.float32(0.0))
         base = jnp.where(c == 1, nb, jnp.where(c == 3, pb, 0))
-        acc = add(acc, jnp.where(c == 3, main + 1, main), base, jnp.where(c == 3, 1, 0), factor)
+        acc = add(acc, jnp.where(c == 3, edge_b, edge_a), base, jnp.where(c == 3, 1, 0), factor)
         store(to_next, c, acc[:, 0:TW])
         store(to_prev, c, acc[:, TW : 2 * TW])
 
@@ -372,17 +403,22 @@
 
         return 0
 
-    lax.fori_loop(0, 5, far, 0)
-
-    def near(j, _):
+    def near(j, _, part=0):
         acc = None
-        for k in range(tiles):
-            part = dot_nt(left(k, rows + 4 * j), hilo[k, 0, 0 : 2 * count, :])
-            acc = part if acc is None else acc + part
-        store(total, j, acc)
-        return 0
-
-    lax.fori_loop(0, 4, near, 0)
+        for k in range(part * (part_k + 1), (part + 1) * (part_k + 1)):
+            piece = dot_nn(left(k, rows + 4 * j), hilo[k, 0, :, 0 : 2 * count])
+            acc = piece if acc is None else acc + piece
+        store(total, j, acc, part == 1)
+        return 0
+
+    for part in range(2):
+        own[part].wait()
+        for copy in copies[part * (groups - 1) : (part + 1) * (groups - 1)]:
+            copy.wait()
+        lax.fori_loop(part * (part_k + 1), (part + 1) * (part_k + 1), centre, 0)
+        if part == 1:
+            lax.fori_loop(0, 5, far, 0)
+        lax.fori_loop(0, 4, functools.partial(near, part=part), 0)
     for c in range(4):
         ahead_copy(c).wait()
         behind_copy(c).wait()
@@ -403,17 +439,36 @@
     tiles = packed_rows // 2
     count = 8 * groups
     tables = [x.reshape(-1, TW) for x in (cells, values, noises)]
+    big = [
+        pltpu.with_memory_space_constraint(x, pltpu.HBM)
+        for x in (members, flow_east, flow_north, mixing, land, lists, counts.reshape(1, rows))
+    ]
+    tables = [pltpu.with_memory_space_constraint(x, pltpu.HBM) for x in tables]
     dma = pltpu.SemaphoreType.DMA
+    far_in = pl.BlockSpec(memory_space=pltpu.HBM)
     return pl.pallas_call(
         functools.partial(cycle_kernel, strips, groups),
         name="cycle",
         out_shape=[
-            jax.ShapeDtypeStruct((packed_rows, count, TW), f32),
+            jax.ShapeDtypeStruct((tiles, count, 2 * TW), f32),
+            jax.ShapeDtypeStruct((tiles, 2 * TW), f32),
             jax.ShapeDtypeStruct((4, count + 8, 4 * count), f32),
         ],
-        in_specs=[pl.BlockSpec(memory_space=VMEM)] * 10,
-        out_specs=[pl.BlockSpec(memory_space=VMEM)] * 2,
+        in_specs=[far_in] * 10,
+        out_specs=[pl.BlockSpec(memory_space=VMEM)] * 3,
         scratch_shapes=[
+            VMEM(members.shape, f32),
+            VMEM((rows, width), f32),
+            VMEM((rows, width), f32),
+            VMEM((rows, width), f32),
+            VMEM((rows, width), i32),
+            VMEM(lists.shape, i32),
+            VMEM((1, rows), i32),
+            VMEM(tables[0].shape, i32),
+            VMEM(tables[1].shape, f32),
+            VMEM(tables[2].shape, f32),
+            VMEM((packed_rows, count, TW), f32),
+            VMEM((rows + 2 * STEPS, 8, width), f32),
             VMEM((rows + 2 * STEPS, 8, width), f32),
             VMEM((rows + 2 * STEPS, 8, width), f32),
             VMEM((rows + 6, 4, width), f32),
@@ -425,24 +480,23 @@
             VMEM((3 * rows, slots), f32),
             VMEM((3 * rows, tiles, 2 * TW), f32),
             VMEM((3 * rows, tiles, 2 * TW), f32),
-            VMEM((tiles, count, 2 * TW), f32),
-            VMEM((tiles, 2 * TW), f32),
-            VMEM((tiles, 2, 4 * count, 2 * TW), bf16),
+            VMEM((tiles, 2, 2 * TW, 4 * count), bf16),
             VMEM((5, count + 8, 4 * count), f32),
             VMEM((5, count + 8, 4 * count), f32),
             VMEM((2, 4, count + 8, 4 * count), f32),
-            dma((6,)), dma((6,)), dma((groups - 1,)), dma((groups - 1,)), dma,
+            dma((10,)), dma((6,)), dma((6,)), dma((2 * (groups - 1),)), dma((2 * (groups - 1),)), dma((2,)),
             dma((4,)), dma((4,)), dma((4,)), dma((4,)),
         ],
         compiler_params=pltpu.CompilerParams(
             collective_id=0, has_side_effects=True, vmem_limit_bytes=40 * 1024 * 1024
         ),
-    )(members, flow_east, flow_north, mixing, land, lists, counts, *tables)
-
-
-def analysis_kernel(gram, window, out, zs, rs, scales):
+    )(*big, *tables)
+
+
+def analysis_kernel(gram, centred, means, out, zs, rs, scales):
     quads, count, lanes = zs.shape
     per = lanes // count
+    part_k = (centred.shape[0] - 2) // 2
     row_of = lax.broadcasted_iota(i32, (count, lanes), 0)
     lane_of = lax.broadcasted_iota(i32, (count, lanes), 1)
     eye = jnp.where(row_of == lane_of % count, 1.0, 0.0).astype(f32)
@@ -450,6 +504,7 @@
     seg_col = lax.broadcasted_iota(i32, (lanes, lanes), 1) // count
     diag = seg_row == seg_col
     diag_one = jnp.where(diag, 1.0, 0.0).astype(bf16)
+    every = range(quads)
 
     def blocked(x):
         return jnp.where(diag, jnp.concatenate([x] * per, axis=0), jnp.zeros((), bf16))
@@ -463,66 +518,72 @@
         p = dot_nn(jnp.concatenate([ah, al], axis=0), bh)
         return p[:n] + p[n:] + dot_nn(ah, bl)
 
-    for g in range(quads):
-        b = eye + gram[g, 0:count, :] / (count - 1)
-        sq = jnp.sum(b * b, axis=0, keepdims=True)
+    b = [eye + gram[g, 0:count, :] / (count - 1) for g in every]
+    stacked = []
+    for g in every:
+        sq = jnp.sum(b[g] * b[g], axis=0, keepdims=True)
         h1 = sq.astype(bf16)
         rest = sq - h1.astype(f32)
         h2 = rest.astype(bf16)
         h3 = (rest - h2.astype(f32)).astype(bf16)
-        stacked = jnp.concatenate([jnp.broadcast_to(h, (16, lanes)) for h in (h1, h2, h3)], axis=0)
-        sums = dot_nn(stacked, diag_one)
-        frob = jnp.sqrt(sums[0:1] + sums[16:17] + sums[32:33])
-        z = b / frob
+        stacked += [jnp.broadcast_to(h, (16, lanes)) for h in (h1, h2, h3)]
+    sums = dot_nn(jnp.concatenate(stacked, axis=0), diag_one)
+    z, f = [], []
+    for g in every:
+        at = 48 * g
+        frob = jnp.sqrt(sums[at : at + 1] + sums[at + 16 : at + 17] + sums[at + 32 : at + 33])
+        z.append(b[g] / frob)
         scales[pl.ds(g, 1), :] = jnp.sqrt(frob)
-        f = 1.5 * eye - 0.5 * z
-        rs[g] = f
-        zs[g] = mul(split(f), right(split(z)))
+        f.append(1.5 * eye - 0.5 * z[g])
+        rs[g] = f[g]
+    zr = [right(split(z[g])) for g in every]
+    for g in every:
+        zs[g] = mul(split(f[g]), zr[g])
 
     def step(i, _):
-        for g in range(quads):
-            r, zr = split(rs[g]), right(split(zs[g]))
-            f = split(1.5 * eye - 0.5 * mul(r, zr))
-            zs[g] = mul(f, zr)
-            rs[g] = mul(f, right(r))
+        r = [split(rs[g]) for g in every]
+        z = [split(zs[g]) for g in every]
+        zr = [right(z[g]) for g in every]
+        f = [right(split(1.5 * eye - 0.5 * mul(r[g], zr[g]))) for g in every]
+        for g in every:
+            p = dot_nn(jnp.concatenate([z[g][0], z[g][1], r[g][0], r[g][1]], axis=0), f[g][0])
+            q = dot_nn(jnp.concatenate([z[g][0], r[g][0]], axis=0), f[g][1])
+            zs[g] = p[:count] + p[count : 2 * count] + q[:count]
+            rs[g] = p[2 * count : 3 * count] + p[3 * count :] + q[count:]
         return 0
 
     lax.fori_loop(0, NSITER - 2, step, 0)
     low_half = lax.broadcasted_iota(i32, (count, 2 * count), 1) < count
-
-    for g in range(quads):
-        r = split(rs[g])
-        f = split(1.5 * eye - 0.5 * mul(r, right(split(zs[g]))))
-        t = mul(f, right(r)) / scales[pl.ds(g, 1), :]
-        tr = right(split(t))
-        vec = jnp.broadcast_to(gram[g, count : count + 1, :], (16, lanes))
-        vec = mul(split(vec), tr)
-        vec = mul(split(vec), tr) / (count - 1)
-        mix = t + vec[0:1]
+    r = [split(rs[g]) for g in every]
+    zr = [right(split(zs[g])) for g in every]
+    f = [right(split(1.5 * eye - 0.5 * mul(r[g], zr[g]))) for g in every]
+    t = [mul(r[g], f[g]) / scales[pl.ds(g, 1), :] for g in every]
+    tr = [right(split(t[g])) for g in every]
+    vec = [jnp.broadcast_to(gram[g, count : count + 1, :], (16, lanes)) for g in every]
+    vec = [mul(split(vec[g]), tr[g]) for g in every]
+    vec = [mul(split(vec[g]), tr[g]) / (count - 1) for g in every]
+    for g in every:
+        mix = t[g] + vec[g][0:1]
         for h in range(per // 2):
             two = mix[:, h * 2 * count : (h + 1) * 2 * count]
-            row0 = per * g + 2 * h
-            fields, averages = [], []
-            for q in range(2):
-                x = window[row0 + q]
-                mean = jnp.sum(x, axis=0, keepdims=True) * (1.0 / count)
-                fields.append(x - mean)
-                averages.append(mean)
-            x = split(jnp.concatenate(fields, axis=0))
+            pair = g * (per // 2) + h
+            k = pair + pair // part_k
+            x = split(jnp.concatenate([centred[k, :, 0:TW], centred[k, :, TW : 2 * TW]], axis=0))
             lhs = jnp.concatenate([jnp.where(low_half, two, 0.0), jnp.where(low_half, 0.0, two)], axis=0)
             y = mul(split(lhs), x)
             for q in range(2):
-                out[:, row0 + q, :] = averages[q] + y[q * count : (q + 1) * count]
-
-
-def analyse(gram, window, rows):
+                average = means[k : k + 1, q * TW : (q + 1) * TW]
+                out[:, 2 * pair + q, :] = average + y[q * count : (q + 1) * count]
+
+
+def analyse(gram, centred, means, rows):
     quads, _, lanes = gram.shape
-    count = window.shape[1]
+    count = centred.shape[1]
     return pl.pallas_call(
         analysis_kernel,
         name="analysis",
         out_shape=jax.ShapeDtypeStruct((count, rows, TW), f32),
-        in_specs=[pl.BlockSpec(memory_space=VMEM)] * 2,
+        in_specs=[pl.BlockSpec(memory_space=VMEM)] * 3,
         out_specs=pl.BlockSpec(memory_space=VMEM),
         scratch_shapes=[
             VMEM((quads, count, lanes), f32),
@@ -530,16 +591,16 @@
             VMEM((quads, lanes), f32),
         ],
         compiler_params=pltpu.CompilerParams(vmem_limit_bytes=16 * 1024 * 1024),
-    )(gram, window)
+    )(gram, centred, means)
 
 
 def body(strips, groups, members, flow_east, flow_north, mixing, land_mask, sensor_cell,
          sensor_value, sensor_noise, tile_lists, tile_counts):
-    window, total = cycle(
+    centred, means, total = cycle(
         members, flow_east, flow_north, mixing, land_mask, tile_lists, tile_counts,
         sensor_cell, sensor_value, sensor_noise, strips, groups,
     )
-    return analyse(total, window, members.shape[1])
+    return analyse(total, centred, means, members.shape[1])
 
 
 def solution(mesh):

time: 66.5 us -> 50.4 us (0.76)
  Pallas kernels: 58.7 us -> 50.2 us
  local copies, waits for them, and re-layouts: 7.26 us -> 0 us
    unnamed x19 -> x0, local copies, waits for them, and re-layouts: 7.26 us -> none
    pallas_call x1, Pallas kernels: 11.4 us -> 6.21 us  [analyse(): pl.pallas_call(analysis_kernel, name='analysis', out_shape=jax.ShapeDtype...]
    pallas_call x1, Pallas kernels: 47.3 us -> 44 us  [cycle(): pl.pallas_call(functools.partial(cycle_kernel, strips, groups), name='cyc...]
where the time goes in v3:
time: 50.4 us; the launch traced here: 50.2 us
  Pallas kernels  50.2 us (100%)
    pallas_call x1, Pallas kernels, cycle(): pl.pallas_call(functools.partial(cycle_kernel, strips, groups), name='cyc...  44 us
    pallas_call x1, Pallas kernels, analyse(): pl.pallas_call(analysis_kernel, name='analysis', out_shape=jax.ShapeDtype...  6.21 us

profile of v3, /device:TPU:1, one launch (start us, length us, event | category | flops | bytes accessed | tf_op | source)
XLA Modules:
  0.0 50.2 jit_solution(2912178291104719813)
XLA Ops:
  0.0 44.0 %cycle.1 = (f32[10,64,256]{2,1,0:T(8,128)S(1)}, f32[10,256]{1,0:T(8,128)S(1)}, f32[4,72,256]{2,1,0:T(8,128)S(1)}) custom-call(f32[8,16,1024]{2,1,0:T(8,128)} %members_h.1, f32[16,1024]{1,0:T(8,128)} %east_h.1, f32[16,1024]{1,0:T(8,128)} %north_h.1, f32[16,1024]{1,0:T(8,128)} %mixing_h.1, s32[16,1024]{1,0:T(8,128)} %land_h.1, s32[16,1,256]{2,1,0:T(1,128)} %lists_h.1, ...), custom_call_target="tpu_custom_call" | custom-call | tf_op jit(solution)/shard_map/cycle/pallas_call | solution.py:449
  44.0 6.2 %analysis.1 = f32[64,16,128]{2,1,0:T(8,128)} custom-call(f32[4,72,256]{2,1,0:T(8,128)S(1)} %get-tuple-element.8.gram, f32[10,64,256]{2,1,0:T(8,128)S(1)} %get-tuple-element.9.centred, f32[10,256]{1,0:T(8,128)S(1)} %get-tuple-element.10.means), custom_call_target="tpu_custom_call" | custom-call | tf_op jit(solution)/shard_map/analysis/pallas_call | solution.py:582

commit v4 on v3

--- a/solution.py
+++ b/solution.py
@@ -49,7 +49,7 @@
     centred, means, total,
     members, flow_east, flow_north, mixing, land, tile_lists, tile_counts, cells, values, noises,
     window, buf0, buf1, buf2, coef, outbox, lists, place_ref, row_ref, w_ref, u_ref,
-    weight, forced, hilo, to_next, to_prev, got,
+    weight, forced, hilo, to_next, to_prev, got, next_force, prev_force, got_force,
     load_sem, halo_send, halo_recv, mem_send, mem_recv, own_sem,
     next_send, next_recv, prev_send, prev_recv,
 ):
@@ -230,23 +230,18 @@
 
         lax.fori_loop(0, (rows - 2 - 2 * step) // 2, inner, 0)
 
-    for copy in halo:
+    for copy in halo[:4]:
         copy.wait_recv()
 
     @pl.when(s == 0)
     def _():
         buf0[pl.ds(0, STEPS)] = jnp.zeros((STEPS, 8, width), f32)
         coef[pl.ds(0, 3)] = jnp.zeros((3, 4, width), f32)
-        lists[pl.ds(0, rows)] = jnp.full((rows, slots), -(1 << 20), i32)
 
     @pl.when(s == strips - 1)
     def _():
         buf0[pl.ds(last, STEPS)] = jnp.zeros((STEPS, 8, width), f32)
         coef[pl.ds(3 + rows, 3)] = jnp.zeros((3, 4, width), f32)
-        lists[pl.ds(2 * rows, rows)] = jnp.full((rows, slots), -(1 << 20), i32)
-
-    for copy in halo:
-        copy.wait_send()
 
     for step in range(STEPS - 1):
         src, dst = chain[step], chain[step + 1]
@@ -256,7 +251,7 @@
             dst[high + i] = advance(src, high + i)
             return 0
 
-        lax.fori_loop(0, STEPS, outer, 0)
+        lax.fori_loop(0, STEPS, outer, 0, unroll=2)
     src = chain[STEPS - 1]
     lane = lax.broadcasted_iota(i32, (8, TW), 1)
 
@@ -295,6 +290,20 @@
         own.append(pltpu.make_async_copy(outbox.at[m, here], mine, own_sem.at[part]))
         own[part].start()
 
+    for copy in halo[4:]:
+        copy.wait_recv()
+
+    @pl.when(s == 0)
+    def _():
+        lists[pl.ds(0, rows)] = jnp.full((rows, slots), -(1 << 20), i32)
+
+    @pl.when(s == strips - 1)
+    def _():
+        lists[pl.ds(2 * rows, rows)] = jnp.full((rows, slots), -(1 << 20), i32)
+
+    for copy in halo:
+        copy.wait_send()
+
     def attributes_far(i, _):
         attributes(2 * i)
         return 0
@@ -317,119 +326,150 @@
         means[pl.ds(k, 1), :] = mean
         high = x.astype(bf16).astype(f32)
         both = jnp.concatenate([high, x - high], axis=0).T.astype(bf16)
-        zero = jnp.zeros((2 * TW, 2 * count), bf16)
-        hilo[k, 0, :, 0 : 2 * count] = both
-        hilo[k, 0, :, 2 * count : 4 * count] = zero
-        hilo[k, 1, :, 0 : 2 * count] = zero
-        hilo[k, 1, :, 2 * count : 4 * count] = both
+        hilo[k] = both
         return 0
 
-    def left(k, base, factor=None):
+    def left(k, base):
         x = centred[k]
         mean = means[pl.ds(k, 1), :]
         pieces, vectors = [], []
         for q in range(4):
             w = weight[base + q, pl.ds(k, 1), :]
-            u = forced[base + q, pl.ds(k, 1), :]
-            if factor is not None:
-                w = w * factor
-                u = u * factor
-            high, low = split(x * w)
-            pieces += [high, low]
-            vectors.append(u - w * mean)
+            pieces += split(x * w)
+            vectors.append(forced[base + q, pl.ds(k, 1), :] - w * mean)
         v = jnp.concatenate(vectors + [jnp.zeros((4, 2 * TW), f32)], axis=0)
         top = v.astype(bf16).astype(f32)
-        pieces.append(jnp.concatenate([top, v - top], axis=0).astype(bf16))
-        return jnp.concatenate(pieces, axis=0)
+        tail = jnp.concatenate([top, v - top], axis=0).astype(bf16)
+        return jnp.concatenate(pieces + [tail], axis=0)
 
     low_half = lax.broadcasted_iota(i32, (count, TW), 1) < count
     low_row = lax.broadcasted_iota(i32, (1, TW), 1) < count
-
-    def store(ref, at, acc, more=False):
-        def put(dst, value):
-            ref[dst] = ref[dst] + value if more else value
-
+    quarter = count // 2
+    upper = (lax.broadcasted_iota(i32, (quarter, TW), 1) & quarter) > 0
+
+    def partial_sums(base, need):
+        acc = None
+        for k in need:
+            part = dot_nn(left(k, base), hilo[k])
+            acc = part if acc is None else acc + part
         folded = []
         for q in range(4):
             x = acc[2 * q * count : (2 * q + 1) * count] + acc[(2 * q + 1) * count : (2 * q + 2) * count]
             folded.append(x + pltpu.roll(x, count, 1))
         v = acc[8 * count : 8 * count + 8] + acc[8 * count + 8 : 8 * count + 16]
         v = v + pltpu.roll(v, count, 1)
+        squares, rows_of = [], []
         for h in range(2):
-            lanes = slice(h * TW, (h + 1) * TW)
-            put((at, slice(0, count), lanes), jnp.where(low_half, folded[2 * h], folded[2 * h + 1]))
-            row = jnp.where(low_row, v[2 * h : 2 * h + 1], v[2 * h + 1 : 2 * h + 2])
-            put((at, slice(count, count + 8), lanes), jnp.broadcast_to(row, (8, TW)))
+            squares.append(jnp.where(low_half, folded[2 * h], folded[2 * h + 1]))
+            rows_of.append(jnp.where(low_row, v[2 * h : 2 * h + 1], v[2 * h + 1 : 2 * h + 2]))
+        return squares, rows_of
 
     main = rows // 2
     part_k = main // 2
     edge_a, edge_b = part_k, 2 * part_k + 1
 
+    def near(j, _, part=0):
+        squares, rows_of = partial_sums(
+            rows + 4 * j, range(part * (part_k + 1), (part + 1) * (part_k + 1))
+        )
+        for h in range(2):
+            lanes = slice(h * TW, (h + 1) * TW)
+            wide = jnp.broadcast_to(rows_of[h], (8, TW))
+            if part == 0:
+                total[j, 0:count, lanes] = squares[h]
+                total[j, count : count + 8, lanes] = wide
+            else:
+                total[j, 0:count, lanes] += squares[h]
+                total[j, count : count + 8, lanes] += wide
+        return 0
+
+    def far(c, base, need, out, out_force):
+        squares, rows_of = partial_sums(base, need)
+        for h in range(2):
+            lanes = slice(h * TW, (h + 1) * TW)
+            out[c, 0:quarter, lanes] = squares[h][0:quarter]
+            out_force[c : c + 1, lanes] = rows_of[h]
+        last_part = jnp.where(upper, squares[0][quarter:], pltpu.roll(squares[1][quarter:], TW - quarter, 1))
+        out[c, quarter : quarter + quarter // 2, 0:TW] = last_part[: quarter // 2]
+        out[c, quarter : quarter + quarter // 2, TW : 2 * TW] = last_part[quarter // 2 :]
+
     def ahead_copy(c):
         return to(c, to_next.at[c], got.at[0, c], nxt, next_send, next_recv)
 
     def behind_copy(c):
-        return to(c, to_prev.at[c + 1], got.at[1, c], prv, prev_send, prev_recv)
-
-    def far(c, _):
-        nb = 2 * rows + 4 * c
-        pb = 4 * (c - 1)
-        acc = None
-
-        def add(acc, k, base, sel, factor=None):
-            part = dot_nn(left(k, base, factor), hilo[k, sel])
-            return part if acc is None else acc + part
-
-        for k in range(main):
-            ahead = 2 * c <= k
-            acc = add(acc, k + k // part_k, jnp.where(ahead, nb, pb), jnp.where(ahead, 0, 1))
-        ahead = c < 4
-        acc = add(acc, edge_b, jnp.where(ahead, nb, pb), jnp.where(ahead, 0, 1))
-        behind = c >= 1
-        acc = add(acc, edge_a, jnp.where(behind, pb, nb), jnp.where(behind, 1, 0))
-        factor = jnp.where((c == 1) | (c == 3), jnp.float32(1.0), jnp.float32(0.0))
-        base = jnp.where(c == 1, nb, jnp.where(c == 3, pb, 0))
-        acc = add(acc, jnp.where(c == 3, edge_b, edge_a), base, jnp.where(c == 3, 1, 0), factor)
-        store(to_next, c, acc[:, 0:TW])
-        store(to_prev, c, acc[:, TW : 2 * TW])
-
-        @pl.when(c < 4)
-        def _():
-            ahead_copy(c).start()
-
-        @pl.when(c >= 1)
-        def _():
-            behind_copy(c - 1).start()
-
-        return 0
-
-    def near(j, _, part=0):
-        acc = None
-        for k in range(part * (part_k + 1), (part + 1) * (part_k + 1)):
-            piece = dot_nn(left(k, rows + 4 * j), hilo[k, 0, :, 0 : 2 * count])
-            acc = piece if acc is None else acc + piece
-        store(total, j, acc, part == 1)
-        return 0
+        return to(c, to_prev.at[c], got.at[1, c], prv, prev_send, prev_recv)
+
+    ahead_force = to(4, next_force, got_force.at[0], nxt, next_send, next_recv)
+    behind_force = to(4, prev_force, got_force.at[1], prv, prev_send, prev_recv)
+    next_force[...] = jnp.zeros(next_force.shape, f32)
+    prev_force[...] = jnp.zeros(prev_force.shape, f32)
+
+    def at_k(k):
+        return k + k // part_k
+
+    def ahead(c):
+        need = [at_k(k) for k in range(2 * c, main)]
+        need += [edge_a, edge_b] if c < 2 else [edge_b]
+        far(c, 2 * rows + 4 * c, need, to_next, next_force)
+
+    def behind(c):
+        need = [at_k(k) for k in range(0, 2 * c + 2)]
+        need += [edge_a] if c < 2 else [edge_a, edge_b]
+        far(c, 4 * c, need, to_prev, prev_force)
 
     for part in range(2):
         own[part].wait()
         for copy in copies[part * (groups - 1) : (part + 1) * (groups - 1)]:
             copy.wait()
-        lax.fori_loop(part * (part_k + 1), (part + 1) * (part_k + 1), centre, 0)
-        if part == 1:
-            lax.fori_loop(0, 5, far, 0)
-        lax.fori_loop(0, 4, functools.partial(near, part=part), 0)
+        first = part * (part_k + 1)
+        lax.fori_loop(first, first + part_k + 1, centre, 0, unroll=part_k + 1)
+        if part == 0:
+            behind(0)
+            behind(1)
+            behind_copy(0).start()
+            behind_copy(1).start()
+        else:
+            ahead(3)
+            ahead(2)
+            ahead_copy(3).start()
+            ahead_copy(2).start()
+            ahead(1)
+            behind(2)
+            ahead_copy(1).start()
+            behind_copy(2).start()
+            ahead(0)
+            behind(3)
+            ahead_copy(0).start()
+            ahead_force.start()
+            behind_copy(3).start()
+            behind_force.start()
+        lax.fori_loop(0, 4, functools.partial(near, part=part), 0, unroll=2)
     for c in range(4):
         ahead_copy(c).wait()
         behind_copy(c).wait()
-
-    @pl.when(s > 0)
-    def _():
-        total[...] += got[0]
-
-    @pl.when(s < strips - 1)
-    def _():
-        total[...] += got[1]
+    ahead_force.wait()
+    behind_force.wait()
+
+    def both(ref, at):
+        return jnp.where(s > 0, ref[(0, *at)], 0.0) + jnp.where(s < strips - 1, ref[(1, *at)], 0.0)
+
+    more = both(got_force, (slice(0, 8), slice(0, 2 * TW)))
+    blank = jnp.zeros((quarter, TW), f32)
+    for g in range(4):
+        extra = both(got, (g,))
+        packed = jnp.concatenate(
+            [extra[quarter : quarter + quarter // 2, 0:TW], extra[quarter : quarter + quarter // 2, TW:]], axis=0
+        )
+        for h in range(2):
+            lanes = slice(h * TW, (h + 1) * TW)
+            top = extra[0:quarter, lanes]
+            turned = jnp.concatenate(
+                [pltpu.roll(top, TW - quarter, 1), blank, pltpu.roll(top, quarter, 1), blank], axis=0
+            ).T[0:quarter]
+            corner = packed if h == 0 else pltpu.roll(packed, quarter, 1)
+            total[g, 0:quarter, lanes] += top
+            total[g, quarter:count, lanes] += jnp.where(upper, corner, turned)
+            total[g, count : count + 8, lanes] += jnp.broadcast_to(more[g : g + 1, lanes], (8, TW))
 
 
 def cycle(members, flow_east, flow_north, mixing, land, lists, counts, cells, values, noises, strips, groups):
@@ -480,12 +520,15 @@
             VMEM((3 * rows, slots), f32),
             VMEM((3 * rows, tiles, 2 * TW), f32),
             VMEM((3 * rows, tiles, 2 * TW), f32),
-            VMEM((tiles, 2, 2 * TW, 4 * count), bf16),
-            VMEM((5, count + 8, 4 * count), f32),
-            VMEM((5, count + 8, 4 * count), f32),
-            VMEM((2, 4, count + 8, 4 * count), f32),
+            VMEM((tiles, 2 * TW, 2 * count), bf16),
+            VMEM((4, 3 * count // 4, 4 * count), f32),
+            VMEM((4, 3 * count // 4, 4 * count), f32),
+            VMEM((2, 4, 3 * count // 4, 4 * count), f32),
+            VMEM((8, 4 * count), f32),
+            VMEM((8, 4 * count), f32),
+            VMEM((2, 8, 4 * count), f32),
             dma((10,)), dma((6,)), dma((6,)), dma((2 * (groups - 1),)), dma((2 * (groups - 1),)), dma((2,)),
-            dma((4,)), dma((4,)), dma((4,)), dma((4,)),
+            dma((5,)), dma((5,)), dma((5,)), dma((5,)),
         ],
         compiler_params=pltpu.CompilerParams(
             collective_id=0, has_side_effects=True, vmem_limit_bytes=40 * 1024 * 1024
@@ -552,7 +595,7 @@
             rs[g] = p[2 * count : 3 * count] + p[3 * count :] + q[count:]
         return 0
 
-    lax.fori_loop(0, NSITER - 2, step, 0)
+    lax.fori_loop(0, NSITER - 2, step, 0, unroll=3)
     low_half = lax.broadcasted_iota(i32, (count, 2 * count), 1) < count
     r = [split(rs[g]) for g in every]
     zr = [right(split(zs[g])) for g in every]

time: 50.4 us -> 47.4 us (0.940)
  Pallas kernels: 50.2 us -> 47.3 us
    pallas_call x1, Pallas kernels: 44 us -> 41.5 us  [cycle(): pl.pallas_call(functools.partial(cycle_kernel, strips, groups), name='cyc...]
where the time goes in v4:
time: 47.4 us; the launch traced here: 47.3 us
  Pallas kernels  47.3 us (100%)
    pallas_call x1, Pallas kernels, cycle(): pl.pallas_call(functools.partial(cycle_kernel, strips, groups), name='cyc...  41.5 us
    pallas_call x1, Pallas kernels, analyse(): pl.pallas_call(analysis_kernel, name='analysis', out_shape=jax.ShapeDtype...  5.75 us

profile of v4, /device:TPU:1, one launch (start us, length us, event | category | flops | bytes accessed | tf_op | source)
XLA Modules:
  0.0 47.3 jit_solution(550230946903471698)
XLA Ops:
  0.0 41.5 %cycle.1 = (f32[10,64,256]{2,1,0:T(8,128)S(1)}, f32[10,256]{1,0:T(8,128)S(1)}, f32[4,72,256]{2,1,0:T(8,128)S(1)}) custom-call(f32[8,16,1024]{2,1,0:T(8,128)} %members_h.1, f32[16,1024]{1,0:T(8,128)} %east_h.1, f32[16,1024]{1,0:T(8,128)} %north_h.1, f32[16,1024]{1,0:T(8,128)} %mixing_h.1, s32[16,1024]{1,0:T(8,128)} %land_h.1, s32[16,1,256]{2,1,0:T(1,128)} %lists_h.1, ...), custom_call_target="tpu_custom_call" | custom-call | tf_op jit(solution)/shard_map/cycle/pallas_call | solution.py:489
  41.5 5.7 %analysis.1 = f32[64,16,128]{2,1,0:T(8,128)} custom-call(f32[4,72,256]{2,1,0:T(8,128)S(1)} %get-tuple-element.8.gram, f32[10,64,256]{2,1,0:T(8,128)S(1)} %get-tuple-element.9.centred, f32[10,256]{1,0:T(8,128)S(1)} %get-tuple-element.10.means), custom_call_target="tpu_custom_call" | custom-call | tf_op jit(solution)/shard_map/analysis/pallas_call | solution.py:625

commit v5 on v4

--- a/solution.py
+++ b/solution.py
@@ -12,6 +12,7 @@
 NSITER = 8
 RLOC = 8
 EDGE = 16
+PAIR_AT = (5, 6, 0, 1, 2, 3, 7, 8)
 MESH = pl.DeviceIdType.MESH
 VMEM = pltpu.VMEM
 f32 = jnp.float32
@@ -74,8 +75,19 @@
     per_strip = chunks * TW
     count = 8 * groups
     barrier = pltpu.get_barrier_semaphore()
-    for other in (prv, nxt):
+    has_prev, has_next = s > 0, s < strips - 1
+
+    def when(wanted, actions):
+        @pl.when(wanted)
+        def _():
+            for action in actions:
+                action()
+
+    def greet(other):
         pl.semaphore_signal(barrier, inc=1, device_id={"space": other}, device_id_type=MESH)
+
+    when(has_prev, [lambda: greet(prv)])
+    when(has_next, [lambda: greet(nxt)])
     for step in range(1, groups):
         peer = lax.rem(m + step, groups)
         pl.semaphore_signal(barrier, inc=1, device_id={"mem": peer}, device_id_type=MESH)
@@ -99,7 +111,7 @@
     used = jnp.where(square, jnp.broadcast_to(tile_counts[...].astype(f32), (rows, rows)), 0.0)
     used = jnp.sum(used, axis=1, keepdims=True)
     lists[pl.ds(rows, rows)] = jnp.where(slot.astype(f32) < used, tile_lists[:, 0, :], -(1 << 20))
-    pl.semaphore_wait(barrier, 2 + groups - 1)
+    pl.semaphore_wait(barrier, groups - 1 + has_prev.astype(i32) + has_next.astype(i32))
 
     def to(k, src, dst, other, send=halo_send, recv=halo_recv):
         return pltpu.make_async_remote_copy(
@@ -117,8 +129,9 @@
         to(4, mine_l, lists.at[pl.ds(0, rows)], nxt),
         to(5, mine_l, lists.at[pl.ds(2 * rows, rows)], prv),
     ]
-    for copy in halo:
-        copy.start()
+    ahead_halo, behind_halo = halo[0::2], halo[1::2]
+    when(has_next, [copy.start for copy in ahead_halo])
+    when(has_prev, [copy.start for copy in behind_halo])
     for r in range(STEPS, rows - STEPS):
         fill(r)
 
@@ -192,18 +205,10 @@
             at = 4 * rows + 4 * k
             e = out[at : at + 4, TW:] + out[at + 4 : at + 8, TW:]
             low, high = x[0:half], x[half:rows]
-            part = half // 2
-            ref[t, :, 0:TW] = jnp.concatenate([low[:part], e[0:1], low[part:], e[1:2]], axis=0)
-            ref[t, :, TW : 2 * TW] = jnp.concatenate([high[:part], e[2:3], high[part:], e[3:4]], axis=0)
-
-    attributes(jnp.int32(1))
-
-    def scatter_own(i, _):
-        for q in range(4):
-            scatter(rows + 4 * i + q)
-        return 0
-
-    lax.fori_loop(0, rows // 4, scatter_own, 0)
+            ref[t, :, 0:TW] = jnp.concatenate([low[2:6], e[2:3], low[0:2], low[6:8], e[0:1]], axis=0)
+            ref[t, :, TW : 2 * TW] = jnp.concatenate(
+                [high[2:6], e[1:2], high[0:2], high[6:8], e[3:4]], axis=0
+            )
 
     def advance(src, i):
         c = src[i]
@@ -230,52 +235,30 @@
 
         lax.fori_loop(0, (rows - 2 - 2 * step) // 2, inner, 0)
 
-    for copy in halo[:4]:
-        copy.wait_recv()
-
-    @pl.when(s == 0)
-    def _():
-        buf0[pl.ds(0, STEPS)] = jnp.zeros((STEPS, 8, width), f32)
-        coef[pl.ds(0, 3)] = jnp.zeros((3, 4, width), f32)
-
-    @pl.when(s == strips - 1)
-    def _():
-        buf0[pl.ds(last, STEPS)] = jnp.zeros((STEPS, 8, width), f32)
-        coef[pl.ds(3 + rows, 3)] = jnp.zeros((3, 4, width), f32)
-
-    for step in range(STEPS - 1):
-        src, dst = chain[step], chain[step + 1]
-
-        def outer(i, _, src=src, dst=dst, low=step + 1, high=rows + STEPS - 1 - step):
-            dst[low + i] = advance(src, low + i)
-            dst[high + i] = advance(src, high + i)
-            return 0
-
-        lax.fori_loop(0, STEPS, outer, 0, unroll=2)
-    src = chain[STEPS - 1]
     lane = lax.broadcasted_iota(i32, (8, TW), 1)
 
     packed_rows = window.shape[0]
     chunk = packed_rows // 2
 
-    def final(g, _, shift=0):
+    def final(i, _, part=0):
+        g, base, edges = ((1 + i, 4 * i, 8 + i), (3 * i, 10 + 4 * i, 18 + i))[part]
         packed = [jnp.zeros((8, TW), f32) for _ in range(groups)]
         for q in range(4):
-            r = 4 * g + q
-            value = advance(src, STEPS + r)
+            value = advance(chain[STEPS - 1], STEPS + 4 * g + q)
             blocks = [value[:, b * TW : (b + 1) * TW] for b in range(groups)]
             for b in range(groups):
-                outbox[b, r + shift] = blocks[b]
+                outbox[b, base + q] = blocks[b]
                 both = jnp.where(lane < EDGE, blocks[(b + 1) % groups], blocks[(b - 1) % groups])
                 turned = pltpu.roll(both, (32 * q + EDGE) % TW, 1)
                 packed[b] = jnp.where(lane // 32 == q, turned, packed[b])
         for b in range(groups):
-            outbox[b, rows // 2 + 4 * shift + g] = packed[b]
+            outbox[b, edges] = packed[b]
         return 0
 
     copies, own = [], []
-    for part in range(2):
-        lax.fori_loop(2 * part, 2 * part + 2, functools.partial(final, shift=2 * part), 0)
+
+    def exchange(part):
+        lax.fori_loop(0, 2, functools.partial(final, part=part), 0)
         here = pl.ds(chunk * part, chunk)
         mine = window.at[here, pl.ds(pl.multiple_of(8 * m, 8), 8), :]
         for k, step in enumerate((4, 3, 5, 2, 6, 7, 1)):
@@ -290,8 +273,41 @@
         own.append(pltpu.make_async_copy(outbox.at[m, here], mine, own_sem.at[part]))
         own[part].start()
 
-    for copy in halo[4:]:
-        copy.wait_recv()
+    exchange(0)
+    attributes(jnp.int32(1))
+
+    def scatter_own(i, _):
+        for q in range(4):
+            scatter(rows + 4 * i + q)
+        return 0
+
+    lax.fori_loop(0, rows // 4, scatter_own, 0)
+
+    when(has_prev, [copy.wait_recv for copy in ahead_halo[:2]])
+    when(has_next, [copy.wait_recv for copy in behind_halo[:2]])
+
+    @pl.when(s == 0)
+    def _():
+        buf0[pl.ds(0, STEPS)] = jnp.zeros((STEPS, 8, width), f32)
+        coef[pl.ds(0, 3)] = jnp.zeros((3, 4, width), f32)
+
+    @pl.when(s == strips - 1)
+    def _():
+        buf0[pl.ds(last, STEPS)] = jnp.zeros((STEPS, 8, width), f32)
+        coef[pl.ds(3 + rows, 3)] = jnp.zeros((3, 4, width), f32)
+
+    for step in range(STEPS - 1):
+        src, dst = chain[step], chain[step + 1]
+
+        def outer(i, _, src=src, dst=dst, low=step + 1, high=rows + STEPS - 1 - step):
+            dst[low + i] = advance(src, low + i)
+            dst[high + i] = advance(src, high + i)
+            return 0
+
+        lax.fori_loop(0, STEPS, outer, 0, unroll=2)
+    exchange(1)
+    when(has_prev, [ahead_halo[2].wait_recv])
+    when(has_next, [behind_halo[2].wait_recv])
 
     @pl.when(s == 0)
     def _():
@@ -301,8 +317,8 @@
     def _():
         lists[pl.ds(2 * rows, rows)] = jnp.full((rows, slots), -(1 << 20), i32)
 
-    for copy in halo:
-        copy.wait_send()
+    when(has_next, [copy.wait_send for copy in ahead_halo])
+    when(has_prev, [copy.wait_send for copy in behind_halo])
 
     def attributes_far(i, _):
         attributes(2 * i)
@@ -401,20 +417,24 @@
 
     ahead_force = to(4, next_force, got_force.at[0], nxt, next_send, next_recv)
     behind_force = to(4, prev_force, got_force.at[1], prv, prev_send, prev_recv)
+    for side, absent in enumerate((s == 0, s == strips - 1)):
+
+        @pl.when(absent)
+        def _(side=side):
+            got[side] = jnp.zeros(got.shape[1:], f32)
+            got_force[side] = jnp.zeros(got_force.shape[1:], f32)
+
     next_force[...] = jnp.zeros(next_force.shape, f32)
     prev_force[...] = jnp.zeros(prev_force.shape, f32)
 
-    def at_k(k):
-        return k + k // part_k
-
     def ahead(c):
-        need = [at_k(k) for k in range(2 * c, main)]
-        need += [edge_a, edge_b] if c < 2 else [edge_b]
+        need = [PAIR_AT[p] for p in range(2 * c, main)]
+        need += [edge_a, edge_b] if c < 3 else [edge_b]
         far(c, 2 * rows + 4 * c, need, to_next, next_force)
 
     def behind(c):
-        need = [at_k(k) for k in range(0, 2 * c + 2)]
-        need += [edge_a] if c < 2 else [edge_a, edge_b]
+        need = [PAIR_AT[p] for p in range(0, 2 * c + 2)]
+        need += [edge_b] if c == 0 else [edge_a, edge_b]
         far(c, 4 * c, need, to_prev, prev_force)
 
     for part in range(2):
@@ -423,35 +443,20 @@
             copy.wait()
         first = part * (part_k + 1)
         lax.fori_loop(first, first + part_k + 1, centre, 0, unroll=part_k + 1)
-        if part == 0:
-            behind(0)
-            behind(1)
-            behind_copy(0).start()
-            behind_copy(1).start()
-        else:
-            ahead(3)
-            ahead(2)
-            ahead_copy(3).start()
-            ahead_copy(2).start()
-            ahead(1)
-            behind(2)
-            ahead_copy(1).start()
-            behind_copy(2).start()
-            ahead(0)
-            behind(3)
-            ahead_copy(0).start()
-            ahead_force.start()
-            behind_copy(3).start()
-            behind_force.start()
+        if part == 1:
+            for c in range(4):
+                ahead(3 - c)
+                behind(c)
+                when(has_next, [ahead_copy(3 - c).start] + ([ahead_force.start] if c == 3 else []))
+                when(has_prev, [behind_copy(c).start] + ([behind_force.start] if c == 3 else []))
         lax.fori_loop(0, 4, functools.partial(near, part=part), 0, unroll=2)
-    for c in range(4):
-        ahead_copy(c).wait()
-        behind_copy(c).wait()
-    ahead_force.wait()
-    behind_force.wait()
+    ahead_all = [ahead_copy(c) for c in range(4)] + [ahead_force]
+    behind_all = [behind_copy(c) for c in range(4)] + [behind_force]
+    when(has_next, [copy.wait_send for copy in ahead_all] + [copy.wait_recv for copy in behind_all])
+    when(has_prev, [copy.wait_recv for copy in ahead_all] + [copy.wait_send for copy in behind_all])
 
     def both(ref, at):
-        return jnp.where(s > 0, ref[(0, *at)], 0.0) + jnp.where(s < strips - 1, ref[(1, *at)], 0.0)
+        return ref[(0, *at)] + ref[(1, *at)]
 
     more = both(got_force, (slice(0, 8), slice(0, 2 * TW)))
     blank = jnp.zeros((quarter, TW), f32)
@@ -539,7 +544,6 @@
 def analysis_kernel(gram, centred, means, out, zs, rs, scales):
     quads, count, lanes = zs.shape
     per = lanes // count
-    part_k = (centred.shape[0] - 2) // 2
     row_of = lax.broadcasted_iota(i32, (count, lanes), 0)
     lane_of = lax.broadcasted_iota(i32, (count, lanes), 1)
     eye = jnp.where(row_of == lane_of % count, 1.0, 0.0).astype(f32)
@@ -610,7 +614,7 @@
         for h in range(per // 2):
             two = mix[:, h * 2 * count : (h + 1) * 2 * count]
             pair = g * (per // 2) + h
-            k = pair + pair // part_k
+            k = PAIR_AT[pair]
             x = split(jnp.concatenate([centred[k, :, 0:TW], centred[k, :, TW : 2 * TW]], axis=0))
             lhs = jnp.concatenate([jnp.where(low_half, two, 0.0), jnp.where(low_half, 0.0, two)], axis=0)
             y = mul(split(lhs), x)

time: 47.4 us -> 40.9 us (0.86)
  the two profiles are of different devices: /device:TPU:1 before, /device:TPU:6 now
where the time goes in v5:
time: 40.9 us; the launch traced here: 40.8 us
  Pallas kernels  40.7 us (100%)
    pallas_call x1, Pallas kernels, cycle(): pl.pallas_call(functools.partial(cycle_kernel, strips, groups), name='cyc...  35 us
    pallas_call x1, Pallas kernels, analyse(): pl.pallas_call(analysis_kernel, name='analysis', out_shape=jax.ShapeDtype...  5.74 us

profile of v5, /device:TPU:6, one launch (start us, length us, event | category | flops | bytes accessed | tf_op | source)
XLA Modules:
  0.0 40.8 jit_solution(1747648073579475366)
XLA Ops:
  0.0 35.0 %cycle.1 = (f32[10,64,256]{2,1,0:T(8,128)S(1)}, f32[10,256]{1,0:T(8,128)S(1)}, f32[4,72,256]{2,1,0:T(8,128)S(1)}) custom-call(f32[8,16,1024]{2,1,0:T(8,128)} %members_h.1, f32[16,1024]{1,0:T(8,128)} %east_h.1, f32[16,1024]{1,0:T(8,128)} %north_h.1, f32[16,1024]{1,0:T(8,128)} %mixing_h.1, s32[16,1024]{1,0:T(8,128)} %land_h.1, s32[16,1,256]{2,1,0:T(1,128)} %lists_h.1, ...), custom_call_target="tpu_custom_call" | custom-call | tf_op jit(solution)/shard_map/cycle/pallas_call | solution.py:494
  35.0 5.7 %analysis.1 = f32[64,16,128]{2,1,0:T(8,128)} custom-call(f32[4,72,256]{2,1,0:T(8,128)S(1)} %get-tuple-element.8.gram, f32[10,64,256]{2,1,0:T(8,128)S(1)} %get-tuple-element.9.centred, f32[10,256]{1,0:T(8,128)S(1)} %get-tuple-element.10.means), custom_call_target="tpu_custom_call" | custom-call | tf_op jit(solution)/shard_map/analysis/pallas_call | solution.py:629
